TPU v7x, 256 devices: a whole 4x4x8 slice. The times are simulated.
256 devices in a mesh: dp: 32 (over z, x_hi, core), depth: 8 (over y, x_lo).
Axes of the slice: x: 4 (x_hi: 2, x_lo: 2; x = x_hi * 2 + x_lo), y: 4, z: 8, core: 2. Of those that a mesh axis runs over, the one named last changes fastest.
Arguments:
- volume: bfloat16 [32, 4, 16, 8, 128], P('dp', None, 'depth'), may hold values from -6 to 6
- kernel_one: bfloat16 [32, 4, 3, 3, 3], replicated, may hold values from -0.625 to 0.625
- bias_one: float32 [32], replicated, may hold values from -0.5 to 0.5
- kernel_two: bfloat16 [64, 32, 3, 3, 3], replicated, may hold values from -0.21875 to 0.21875
- bias_two: float32 [64], replicated, may hold values from -0.5 to 0.5
- cotangent: bfloat16 [32, 64, 16, 8, 128], P('dp', None, 'depth'), may hold values from -0.008239746 to 0.008239746
Outputs:
- features: bfloat16 [32, 64, 16, 8, 128], P('dp', None, 'depth')
- grad_kernel_one: float32 [32, 4, 3, 3, 3], replicated
- grad_bias_one: float32 [32], replicated
- grad_kernel_two: float32 [64, 32, 3, 3, 3], replicated
- grad_bias_two: float32 [64], replicated
All inputs are finite; a program needn't handle non-finite values.
Results may differ from a plain program's by a relative error of at most 0.006.
Values may be sent and summed in bfloat16 or wider, within the bound.
No kernel may reach another device: no remote copies, remote signals or barrier semaphores. Data moves between devices by JAX's collectives and lax.ppermute only.
A program may use at most 64 MiB of HBM per device.

v0:
```python
import jax
import jax.numpy as jnp
from jax import lax
from jax.sharding import PartitionSpec as P

FORWARD_DIMS = ("NCDHW", "OIDHW", "NCDHW")
KERNEL_DIMS = ("CNDHW", "IODHW", "CNDHW")


def extended(x, sides, width):
    for axis, dim in sides:
        size, length = (lax.axis_size(axis), x.shape[dim])
        up = [(i, (i + 1) % size) for i in range(size - 1)]
        down = [(j, i) for i, j in up]
        last = lax.slice_in_dim(x, length - width, length, axis=dim)
        leading = lax.slice_in_dim(x, 0, width, axis=dim)
        before = lax.ppermute(last, axis, up)
        after = lax.ppermute(leading, axis, down)
        x = jnp.concatenate([before, x, after], axis=dim)
    return x


def convolve(inputs, kernel, depth_pad=0):
    return lax.conv_general_dilated(
        inputs,
        kernel,
        (1, 1, 1),
        ((depth_pad, depth_pad), (1, 1), (1, 1)),
        dimension_numbers=FORWARD_DIMS,
        preferred_element_type=jnp.float32,
    )


def kernel_grad(inputs, slope):
    return lax.conv_general_dilated(
        inputs,
        slope,
        (1, 1, 1),
        ((0, 0), (1, 1), (1, 1)),
        dimension_numbers=KERNEL_DIMS,
        preferred_element_type=jnp.float32,
    )


def silu_slope(value):
    sig = jax.nn.sigmoid(value)
    return sig * (1.0 + value * (1.0 - sig))


def per_device(volume, kernel_one, bias_one, kernel_two, bias_two, cotangent):
    planes = volume.shape[2]
    shift_one = bias_one[None, :, None, None, None]
    padded = extended(volume, (("depth", 2),), 2)
    pre_wide = convolve(padded, kernel_one) + shift_one
    global_plane = lax.axis_index("depth") * planes + jnp.arange(planes + 2, dtype=jnp.int32) - 1
    inside = (global_plane >= 0) & (global_plane < planes * lax.axis_size("depth"))
    inside = inside.astype(jnp.float32)[None, None, :, None, None]
    act_wide = (jax.nn.silu(pre_wide) * inside).astype(jnp.bfloat16)
    pre_one = pre_wide[:, :, 1:-1]
    input_wide = padded[:, :, 1:-1]
    pre_two = convolve(act_wide, kernel_two) + bias_two[None, :, None, None, None]
    features = jax.nn.silu(pre_two).astype(jnp.bfloat16)
    slope_two = (cotangent.astype(jnp.float32) * silu_slope(pre_two)).astype(jnp.bfloat16)
    grad_two = kernel_grad(act_wide, slope_two)
    bias_grad_two = jnp.sum(slope_two, axis=(0, 2, 3, 4), dtype=jnp.float32)
    flipped = jnp.transpose(jnp.flip(kernel_two, (2, 3, 4)), (1, 0, 2, 3, 4))
    slope_wide = extended(slope_two, (("depth", 2),), 1)
    back_one = convolve(slope_wide, flipped)
    slope_one = (back_one * silu_slope(pre_one)).astype(jnp.bfloat16)
    grad_one = kernel_grad(input_wide, slope_one)
    bias_grad_one = jnp.sum(slope_one, axis=(0, 2, 3, 4), dtype=jnp.float32)
    grad_one, bias_grad_one, grad_two, bias_grad_two = lax.psum(
        (grad_one, bias_grad_one, grad_two, bias_grad_two), ("dp", "depth")
    )
    return (features, grad_one, bias_grad_one, grad_two, bias_grad_two)


def solution(mesh):
    return jax.shard_map(
        per_device,
        mesh=mesh,
        in_specs=(
            P("dp", None, "depth", None, None),
            P(),
            P(),
            P(),
            P(),
            P("dp", None, "depth", None, None),
        ),
        out_specs=(P("dp", None, "depth", None, None), P(), P(), P(), P()),
        check_vma=False,
    )
```

profile of v0, /device:TPU:1, one launch (start us, length us, event | category | flops | bytes accessed | tf_op | source)
XLA Modules:
  0.0 308.6 jit_solution(12884030716695211262)
XLA Ops:
  7.2 4.1 %collective-permute-start = (bf16[1,4,2,8,128]{4,3,2,1,0:T(8,128)(2,1)}, bf16[1,4,2,8,128]{4,3,2,1,0:T(8,128)(2,1)S(1)}, u32[]{:S(2)}, u32[]{:S(2)}) collective-permute-start(bf16[1,4,2,8,128]{4,3,2,1,0:T(8,128)(2,1)} %param.6), channel_id=1, source_target_pairs={{0,1},{1,2},{2,3},{3,4},{4,5},{5,6},{6,7},{8,9},{9,10},{10,11},{11... | collective-permute-start | bytes 49160 | tf_op jit(solution)/shard_map/ppermute | solution.py:17
  11.3 1.3 collective-permute-start.1
  12.6 1.4 copy.76
  14.0 2.0 collective-permute-done.1
  16.0 0.7 maximum_bitcast_fusion.5
  17.1 1.4 copy.69
  18.7 6.8 %fusion.23 = (bf16[4,8,8,17,32]{4,2,3,1,0:T(8,128)(2,1)S(1)}, f32[4,8,8,17,32]{4,2,3,1,0:T(8,128)}) fusion(f32[4]{0:T(128)S(1)} %and_convert_fusion, pred[8,17]{0,1:T(8,128)(4,1)S(1)} %copy-done.12, f32[32]{0:T(128)S(1)} %copy-done.10, bf16[32,4,3,3,3]{0,1,4,3,2:T(4,128)(2,1)S(1)} %copy-done.9, bf16[4,6,8,1,7,2]{4,0,5,2,1,3:T(4,128)(2,1)S(1)} %slice.28, ...), kind=kOutput, calls=%fused_computation.37 | convolution fusion | flops 29002752 | bytes 900376 | tf_op jit(solution)/shard_map/conv_general_dilated | solution.py:24
  25.5 0.7 fusion.54
  26.2 1.3 fusion.53
  27.8 1.1 fusion.56
  28.9 1.1 fusion.57
  29.9 1.1 reshape.62
  31.0 0.9 pad.2
  31.9 2.7 add_multiply_fusion
  35.2 0.8 fusion.55
  37.1 4.8 %fusion.19 = f32[64,32,3,3,3]{0,1,4,3,2:T(8,128)} fusion(bf16[64,2,8,8,17,1]{0,2,4,3,1,5:T(8,128)(2,1)S(1)} %bitcast.75, bf16[4,8,8,17,32,1]{4,2,3,1,0,5:T(8,128)(2,1)S(1)} %get-tuple-element.51, bf16[4,8,8,17,32,1]{4,2,3,1,0,5:T(8,128)(2,1)S(1)} %bitcast.72, bf16[4,8,8,17,32,1]{4,2,3,1,0,5:T(8,128)(2,1)S(1)} %get-tuple-element.50), kind=kOutput, calls=%fused_computation.29 | convolution fusion | flops 221429760 | bytes 1335296 | tf_op jit(solution)/shard_map/conv_general_dilated | solution.py:35
  41.9 4.9 %collective-permute-start.2 = (bf16[1,64,1,8,128]{1,3,4,2,0:T(8,128)(2,1)}, bf16[1,64,1,8,128]{1,3,4,2,0:T(8,128)(2,1)}, u32[]{:S(2)}, u32[]{:S(2)}) collective-permute-start(bf16[1,64,1,8,128]{1,3,4,2,0:T(8,128)(2,1)} %get-tuple-element.36), channel_id=1, source_target_pairs={{0,1},{1,2},{2,3},{3,4},{4,5},{5,6},{6,7},{8,9},{9,10},{10,11},{11... | collective-permute-start | bytes 393224 | tf_op jit(solution)/shard_map/ppermute | solution.py:17
  46.8 1.3 collective-permute-start.3
  48.1 0.6 copy.85
  48.8 1.6 copy.86
  50.4 1.2 copy.84
  51.6 1.9 copy.87
  53.5 2.1 copy.75
  55.8 1.1 copy.83
  56.9 0.9 fusion.33
  57.9 1.3 maximum_bitcast_fusion.4
  59.6 1.4 copy-done.13
  61.0 4.4 %select_reduce_fusion = (f32[32]{0:T(128)S(1)}, bf16[2,8,8,17,32]{4,2,3,1,0:T(8,128)(2,1)S(1)}) fusion(pred[8,17]{0,1:T(8,128)(4,1)S(1)} %copy-done.12, f32[4,8,8,17,32]{4,2,3,1,0:T(8,128)S(1)} %copy-done.13, bf16[64,32,3,3,3]{0,1,4,3,2:T(8,128)(2,1)S(1)} %copy-done, bf16[64,4,8,1,7,2]{0,4,5,2,1,3:T(8,128)(2,1)S(1)} %slice.39, ...), kind=kOutput, calls=%fused_computation.33 | convolution fusion | flops 223367136 | bytes 1143048 | tf_op jit(solution)/shard_map/conv_general_dilated | solution.py:24
  65.4 3.8 %fusion.22 = f32[32,4,3,3,3]{0,1,4,3,2:T(4,128)S(1)} fusion(bf16[4,6,8,8,17,1]{3,0,5,4,2,1:T(4,128)(2,1)S(1)} %get-tuple-element.48, bf16[4,6,8,8,17,1]{3,0,5,4,2,1:T(4,128)(2,1)S(1)} %copy-done.6, bf16[4,6,8,8,17,1]{3,0,5,4,2,1:T(4,128)(2,1)S(1)} %get-tuple-element.49, bf16[2,8,8,17,32]{4,2,3,1,0:T(8,128)(2,1)S(1)} %get-tuple-element.47, ...), kind=kOutput, calls=%fused_computation.30 | convolution fusion | flops 14326784 | bytes 309896 | tf_op jit(solution)/shard_map/conv_general_dilated | solution.py:35
  69.1 82.2 %all-reduce = (f32[32,4,3,3,3]{0,1,4,3,2:T(4,128)}, f32[32]{0:T(128)}, f32[64]{0:T(128)}) all-reduce(f32[32,4,3,3,3]{0,1,4,3,2:T(4,128)S(1)} %fusion.22, f32[32]{0:T(128)S(1)} %get-tuple-element.46, f32[64]{0:T(128)S(1)} %get-tuple-element.28), channel_id=1, replica_groups=mesh['dp'=32,'depth'=8] {'dp','depth'}, use_global_device_ids=true, to_apply=%region_0.1 | all-reduce | flops 3552 | bytes 28416 | tf_op jit(solution)/shard_map/psum | solution.py:72
  151.3 148.7 %all-reduce.3.cloned.1.call-done = f32[64,32,3,3,3]{0,1,4,3,2:T(8,128)} async-done(((f32[64,32,3,3,3]{0,1,4,3,2:T(8,128)}), f32[64,32,3,3,3]{0,1,4,3,2:T(8,128)}) %all-reduce.3.cloned.1.call-update) | async-done | bytes 221200 | tf_op jit(solution)/shard_map/psum | solution.py:72
  300.0 1.8 copy.95
  (47 shorter events, 3.0 us)
Async XLA Ops:
  7.2 24.8 %copy-start = (bf16[64,32,3,3,3]{0,1,4,3,2:T(8,128)(2,1)S(1)}, bf16[64,32,3,3,3]{0,1,4,3,2:T(8,128)(2,1)}, u32[]{:S(2)}) copy-start(bf16[64,32,3,3,3]{0,1,4,3,2:T(8,128)(2,1)} %param.9) | copy-start | bytes 331780
  7.2 292.8 %all-reduce.3.cloned.1.call-start = ((), (), s32[]{:S(2)}) async-start(), calls=%async_computation | async-start | bytes 884736 | tf_op jit(solution)/shard_map/psum | solution.py:72
  7.2 6.8 %collective-permute-start = (bf16[1,4,2,8,128]{4,3,2,1,0:T(8,128)(2,1)}, bf16[1,4,2,8,128]{4,3,2,1,0:T(8,128)(2,1)S(1)}, u32[]{:S(2)}, u32[]{:S(2)}) collective-permute-start(bf16[1,4,2,8,128]{4,3,2,1,0:T(8,128)(2,1)} %param.6), channel_id=1, source_target_pairs={{0,1},{1,2},{2,3},{3,4},{4,5},{5,6},{6,7},{8,9},{9,10},{10,11},{11... | collective-permute-start | bytes 49160 | tf_op jit(solution)/shard_map/ppermute | solution.py:17
  11.3 4.7 %collective-permute-start.1 = (bf16[1,4,2,8,128]{4,3,2,1,0:T(8,128)(2,1)}, bf16[1,4,2,8,128]{4,3,2,1,0:T(8,128)(2,1)S(1)}, u32[]{:S(2)}, u32[]{:S(2)}) collective-permute-start(bf16[1,4,2,8,128]{4,3,2,1,0:T(8,128)(2,1)} %param.6), channel_id=1, source_target_pairs={{1,0},{2,1},{3,2},{4,3},{5,4},{6,5},{7,6},{9,8},{10,9},{11,10},{12... | collective-permute-start | bytes 49160 | tf_op jit(solution)/shard_map/ppermute | solution.py:18
  14.0 4.7 %copy-start.9 = (bf16[32,4,3,3,3]{0,1,4,3,2:T(4,128)(2,1)S(1)}, bf16[32,4,3,3,3]{0,1,4,3,2:T(4,128)(2,1)}, u32[]{:S(2)}) copy-start(bf16[32,4,3,3,3]{0,1,4,3,2:T(4,128)(2,1)} %param.7) | copy-start | bytes 20740
  14.0 4.7 %copy-start.10 = (f32[32]{0:T(128)S(1)}, f32[32]{0:T(128)}, u32[]{:S(2)}) copy-start(f32[32]{0:T(128)} %param.8) | copy-start | bytes 388
  14.0 4.7 %copy-start.12 = (pred[8,17]{0,1:T(8,128)(4,1)S(1)}, pred[8,17]{0,1:T(8,128)(4,1)}, u32[]{:S(2)}) copy-start(pred[8,17]{0,1:T(8,128)(4,1)} %constant.46) | copy-start | bytes 412
  28.9 3.1 copy-start.11
  35.2 1.4 copy-start.1
  37.1 11.1 %copy-start.5 = (bf16[4,6,8,1,8,16]{5,4,2,1,0,3:T(8,128)(2,1)S(1)}, bf16[4,6,8,1,8,16]{5,4,2,1,0,3:T(8,128)(2,1)}, u32[]{:S(2)}) copy-start(bf16[4,6,8,1,8,16]{5,4,2,1,0,3:T(8,128)(2,1)} %get-tuple-element.38) | copy-start | bytes 147460
  41.9 8.5 %copy-start.3 = (bf16[4,6,8,1,7,1]{5,4,2,1,0,3:T(8,128)(2,1)S(1)}, bf16[4,6,8,1,7,1]{5,4,2,1,0,3:T(8,128)(2,1)}, u32[]{:S(2)}) copy-start(bf16[4,6,8,1,7,1]{5,4,2,1,0,3:T(8,128)(2,1)} %get-tuple-element.40) | copy-start | bytes 8068
  41.9 15.9 %collective-permute-start.2 = (bf16[1,64,1,8,128]{1,3,4,2,0:T(8,128)(2,1)}, bf16[1,64,1,8,128]{1,3,4,2,0:T(8,128)(2,1)}, u32[]{:S(2)}, u32[]{:S(2)}) collective-permute-start(bf16[1,64,1,8,128]{1,3,4,2,0:T(8,128)(2,1)} %get-tuple-element.36), channel_id=1, source_target_pairs={{0,1},{1,2},{2,3},{3,4},{4,5},{5,6},{6,7},{8,9},{9,10},{10,11},{11... | collective-permute-start | bytes 393224 | tf_op jit(solution)/shard_map/ppermute | solution.py:17
  46.8 11.0 %collective-permute-start.3 = (bf16[1,64,1,8,128]{1,3,4,2,0:T(8,128)(2,1)}, bf16[1,64,1,8,128]{1,3,4,2,0:T(8,128)(2,1)}, u32[]{:S(2)}, u32[]{:S(2)}) collective-permute-start(bf16[1,64,1,8,128]{1,3,4,2,0:T(8,128)(2,1)} %get-tuple-element.37), channel_id=1, source_target_pairs={{1,0},{2,1},{3,2},{4,3},{5,4},{6,5},{7,6},{9,8},{10,9},{11,10},{12... | collective-permute-start | bytes 393224 | tf_op jit(solution)/shard_map/ppermute | solution.py:18
  48.1 3.5 %copy-start.2 = (bf16[4,6,8,1,7,1]{5,4,2,1,0,3:T(8,128)(2,1)S(1)}, bf16[4,6,8,1,7,1]{5,4,2,1,0,3:T(8,128)(2,1)}, u32[]{:S(2)}) copy-start(bf16[4,6,8,1,7,1]{5,4,2,1,0,3:T(8,128)(2,1)} %get-tuple-element.41) | copy-start | bytes 8068
  48.8 4.7 %copy-start.4 = (bf16[4,6,8,8,17,1]{4,3,2,1,0,5:T(8,128)(2,1)S(1)}, bf16[4,6,8,8,17,1]{4,3,2,1,0,5:T(8,128)(2,1)}, u32[]{:S(2)}) copy-start(bf16[4,6,8,8,17,1]{4,3,2,1,0,5:T(8,128)(2,1)} %reshape.62) | copy-start | bytes 156676
  53.5 2.1 copy-start.7
  55.6 1.3 copy-start.8
  59.4 1.6 copy-start.13
  61.0 4.4 %copy-start.6 = (bf16[4,6,8,8,17,1]{3,0,5,4,2,1:T(4,128)(2,1)S(1)}, bf16[4,6,8,8,17,1]{3,0,5,4,2,1:T(4,128)(2,1)}, u32[]{:S(2)}) copy-start(bf16[4,6,8,8,17,1]{3,0,5,4,2,1:T(4,128)(2,1)} %copy.75) | copy-start | bytes 156676
Sparse Core Ops, SparseCore 0:
  42.0 257.9 all-reduce.2
where the time goes:
time: 309 us
  waiting for transfers between devices  151 us (49%)
  blocking collectives  82.2 us (27%)
  local copies, waits for them, and re-layouts  23.7 us (8%)
  matrix products  22.5 us (7%)
  between operations  14.4 us (5%)
  starting transfers between devices  11.6 us (4%)
  other arithmetic  3.68 us (1%)
    psum x1, waiting for transfers between devices, per_device(): lax.psum((grad_one, bias_grad_one, grad_two, bias_grad_two), ('dp', 'dept...  149 us
    psum x1, blocking collectives, per_device(): lax.psum((grad_one, bias_grad_one, grad_two, bias_grad_two), ('dp', 'dept...  82.2 us
    conv_general_dilated x3, matrix products, convolve(): lax.conv_general_dilated(inputs, kernel, (1, 1, 1), ((depth_pad, depth_pa...  13.9 us
    unnamed x35, local copies, waits for them, and re-layouts  11.6 us
    ppermute x2, starting transfers between devices, extended(): before = lax.ppermute(last, axis, up)  8.99 us
    conv_general_dilated x2, matrix products, kernel_grad(): lax.conv_general_dilated(inputs, slope, (1, 1, 1), ((0, 0), (1, 1), (1, 1...  8.59 us
  transfers between devices with their start and end apart: 5, of which 2 were waited for; matrix products, arithmetic and copies ran while one was open for 7% of the time, Pallas kernels for 0%

commit v1 on v0

--- a/solution.py
+++ b/solution.py
@@ -1,8 +1,13 @@
 import jax
 import jax.numpy as jnp
 from jax import lax
+from jax.sharding import Mesh
 from jax.sharding import PartitionSpec as P
 
+DP = ("z", "x_hi", "core")
+DEPTH = ("y", "x_lo")
+PLANE = ("x_hi", "core", "y", "x_lo")
+LINE = "z"
 FORWARD_DIMS = ("NCDHW", "OIDHW", "NCDHW")
 KERNEL_DIMS = ("CNDHW", "IODHW", "CNDHW")
 
@@ -47,13 +52,29 @@
     return sig * (1.0 + value * (1.0 - sig))
 
 
+def exchange(x, axes):
+    return lax.all_to_all(x, axes, 0, 0, tiled=True)
+
+
+def reduced(x):
+    rows, lanes = x.shape
+    plane = lax.axis_size(PLANE)
+    line = lax.axis_size(LINE)
+    part = exchange(x.reshape(plane, rows // plane, lanes), PLANE)
+    part = jnp.sum(part, axis=0, dtype=jnp.float32).astype(x.dtype)
+    part = exchange(jnp.broadcast_to(part[None], (line,) + part.shape), LINE)
+    part = jnp.sum(part, axis=0, dtype=jnp.float32).astype(x.dtype)
+    part = exchange(jnp.broadcast_to(part[None], (plane,) + part.shape), PLANE)
+    return part.reshape(rows, lanes)
+
+
 def per_device(volume, kernel_one, bias_one, kernel_two, bias_two, cotangent):
     planes = volume.shape[2]
     shift_one = bias_one[None, :, None, None, None]
-    padded = extended(volume, (("depth", 2),), 2)
+    padded = extended(volume, ((DEPTH, 2),), 2)
     pre_wide = convolve(padded, kernel_one) + shift_one
-    global_plane = lax.axis_index("depth") * planes + jnp.arange(planes + 2, dtype=jnp.int32) - 1
-    inside = (global_plane >= 0) & (global_plane < planes * lax.axis_size("depth"))
+    global_plane = lax.axis_index(DEPTH) * planes + jnp.arange(planes + 2, dtype=jnp.int32) - 1
+    inside = (global_plane >= 0) & (global_plane < planes * lax.axis_size(DEPTH))
     inside = inside.astype(jnp.float32)[None, None, :, None, None]
     act_wide = (jax.nn.silu(pre_wide) * inside).astype(jnp.bfloat16)
     pre_one = pre_wide[:, :, 1:-1]
@@ -64,29 +85,34 @@
     grad_two = kernel_grad(act_wide, slope_two)
     bias_grad_two = jnp.sum(slope_two, axis=(0, 2, 3, 4), dtype=jnp.float32)
     flipped = jnp.transpose(jnp.flip(kernel_two, (2, 3, 4)), (1, 0, 2, 3, 4))
-    slope_wide = extended(slope_two, (("depth", 2),), 1)
+    slope_wide = extended(slope_two, ((DEPTH, 2),), 1)
     back_one = convolve(slope_wide, flipped)
     slope_one = (back_one * silu_slope(pre_one)).astype(jnp.bfloat16)
     grad_one = kernel_grad(input_wide, slope_one)
     bias_grad_one = jnp.sum(slope_one, axis=(0, 2, 3, 4), dtype=jnp.float32)
-    grad_one, bias_grad_one, grad_two, bias_grad_two = lax.psum(
-        (grad_one, bias_grad_one, grad_two, bias_grad_two), ("dp", "depth")
-    )
-    return (features, grad_one, bias_grad_one, grad_two, bias_grad_two)
+    two = jnp.transpose(grad_two, (2, 3, 4, 1, 0)).reshape(432, 128)
+    one = jnp.transpose(grad_one, (2, 3, 4, 1, 0)).reshape(27, 128)
+    biases = jnp.concatenate([bias_grad_one, bias_grad_two, jnp.zeros((32,), jnp.float32)]).reshape(1, 128)
+    packed = jnp.concatenate([two, one, biases, jnp.zeros((52, 128), jnp.float32)])
+    total = reduced(packed.astype(jnp.bfloat16)).astype(jnp.float32)
+    grad_two = jnp.transpose(total[:432].reshape(3, 3, 3, 32, 64), (4, 3, 0, 1, 2))
+    grad_one = jnp.transpose(total[432:459].reshape(3, 3, 3, 4, 32), (4, 3, 0, 1, 2))
+    return (features, grad_one, total[459, :32], grad_two, total[459, 32:96])
 
 
 def solution(mesh):
+    cut = Mesh(mesh.devices.reshape(8, 2, 2, 4, 2), DP + DEPTH)
     return jax.shard_map(
         per_device,
-        mesh=mesh,
+        mesh=cut,
         in_specs=(
-            P("dp", None, "depth", None, None),
+            P(DP, None, DEPTH, None, None),
             P(),
             P(),
             P(),
             P(),
-            P("dp", None, "depth", None, None),
+            P(DP, None, DEPTH, None, None),
         ),
-        out_specs=(P("dp", None, "depth", None, None), P(), P(), P(), P()),
+        out_specs=(P(DP, None, DEPTH, None, None), P(), P(), P(), P()),
         check_vma=False,
     )

time: 309 us -> 116 us (0.38)
  waiting for transfers between devices: 151 us -> 13.5 us
  blocking collectives: 82.2 us -> 18.3 us
  starting transfers between devices: 11.6 us -> 26.3 us
  between operations: 14.4 us -> 1.03 us
  local copies, waits for them, and re-layouts: 23.7 us -> 29.5 us
    psum x1 -> x0, waiting for transfers between devices: 149 us -> none  [per_device(): lax.psum((grad_one, bias_grad_one, grad_two, bias_grad_two), ('dp', 'dept...]
    psum x1 -> x0, blocking collectives: 82.2 us -> none  [per_device(): lax.psum((grad_one, bias_grad_one, grad_two, bias_grad_two), ('dp', 'dept...]
    all_to_all x0 -> x1, blocking collectives: none -> 18.3 us  [exchange(): return lax.all_to_all(x, axes, 0, 0, tiled=True)]
    all_to_all x0 -> x2, waiting for transfers between devices: none -> 13.5 us  [exchange(): return lax.all_to_all(x, axes, 0, 0, tiled=True)]
    all_to_all x0 -> x2, starting transfers between devices: none -> 13.5 us  [exchange(): return lax.all_to_all(x, axes, 0, 0, tiled=True)]
    conv_general_dilated x2 -> x0, matrix products: 8.59 us -> none  [kernel_grad(): lax.conv_general_dilated(inputs, slope, (1, 1, 1), ((0, 0), (1, 1), (1, 1...]
    transpose x0 -> x2, matrix products: none -> 8.56 us  [the longest x1 4.57 us: per_device(): two = jnp.transpose(grad_two, (2, 3, 4, 1, 0)).reshape(432, 128)]
    unnamed x35 -> x40, local copies, waits for them, and re-layouts: 11.6 us -> 12.7 us
  transfers between devices with their start and end apart: 5 -> 6, of which waited for: 2 -> 2; matrix products, arithmetic and copies ran while one was open for 7% -> 18% of each run, Pallas kernels for 0% -> 0%
where the time goes in v1:
time: 116 us; the launch traced here: 115 us
  local copies, waits for them, and re-layouts  29.5 us (25%)
  starting transfers between devices  26.3 us (23%)
  matrix products  22.5 us (19%)
  blocking collectives  18.3 us (16%)
  waiting for transfers between devices  13.5 us (12%)
  other arithmetic  3.97 us (3%)
    all_to_all x1, blocking collectives, exchange(): return lax.all_to_all(x, axes, 0, 0, tiled=True)  18.3 us
    conv_general_dilated x3, matrix products, convolve(): lax.conv_general_dilated(inputs, kernel, (1, 1, 1), ((depth_pad, depth_pa...  13.9 us
    all_to_all x2, waiting for transfers between devices, exchange(): return lax.all_to_all(x, axes, 0, 0, tiled=True)  13.5 us
    all_to_all x2, starting transfers between devices, exchange(): return lax.all_to_all(x, axes, 0, 0, tiled=True)  13.5 us
    unnamed x40, local copies, waits for them, and re-layouts  12.7 us
    ppermute x2, starting transfers between devices, extended(): before = lax.ppermute(last, axis, up)  10.2 us
    concatenate x7, local copies, waits for them, and re-layouts, extended(): x = jnp.concatenate([before, x, after], axis=dim)  6.84 us
    transpose x1, matrix products, per_device(): two = jnp.transpose(grad_two, (2, 3, 4, 1, 0)).reshape(432, 128)  4.57 us
  transfers between devices with their start and end apart: 6, of which 2 were waited for; matrix products, arithmetic and copies ran while one was open for 18% of the time, Pallas kernels for 0%

profile of v1, /device:TPU:1, one launch (start us, length us, event | category | flops | bytes accessed | tf_op | source)
XLA Modules:
  0.0 115.1 jit_solution(7057965205918561795)
XLA Ops:
  0.6 1.4 %collective-permute-start.1 = (bf16[1,4,2,8,128]{4,3,2,1,0:T(8,128)(2,1)}, bf16[1,4,2,8,128]{4,3,2,1,0:T(8,128)(2,1)S(1)}, u32[]{:S(2)}, u32[]{:S(2)}) collective-permute-start(bf16[1,4,2,8,128]{4,3,2,1,0:T(8,128)(2,1)} %param.6), channel_id=1, source_target_pairs={{1,0},{2,1},{3,2},{4,3},{5,4},{6,5},{7,6},{9,8},{10,9},{11,10},{12... | collective-permute-start | bytes 49160 | tf_op jit(solution)/shard_map/ppermute | solution.py:23
  2.1 4.6 %collective-permute-start = (bf16[1,4,2,8,128]{4,3,2,1,0:T(8,128)(2,1)}, bf16[1,4,2,8,128]{4,3,2,1,0:T(8,128)(2,1)S(1)}, u32[]{:S(2)}, u32[]{:S(2)}) collective-permute-start(bf16[1,4,2,8,128]{4,3,2,1,0:T(8,128)(2,1)} %param.6), channel_id=1, source_target_pairs={{0,1},{1,2},{2,3},{3,4},{4,5},{5,6},{6,7},{8,9},{9,10},{10,11},{11... | collective-permute-start | bytes 49160 | tf_op jit(solution)/shard_map/ppermute | solution.py:22
  6.7 1.4 %copy.71 = bf16[1,64,2,8,128]{1,3,4,2,0:T(8,128)(2,1)S(1)} copy(bf16[1,64,2,8,128]{4,3,2,1,0:T(8,128)(2,1)} %param.11) | data formatting | bytes 524288 | tf_op args[5]
  9.3 1.1 fusion.58
  10.4 1.0 fusion.57
  11.4 1.1 reshape.94
  12.8 1.4 %copy.69 = bf16[4,6,8,1,8,17]{4,0,5,2,1,3:T(4,128)(2,1)S(1)} copy(bf16[4,6,8,1,8,17]{5,4,2,1,0,3:T(8,128)(2,1)S(1)} %reshape.61) | data formatting | bytes 104448 | tf_op jit(solution)/shard_map/conv_general_dilated | solution.py:29
  14.3 6.8 %fusion.23 = (bf16[4,8,8,17,32]{4,2,3,1,0:T(8,128)(2,1)S(1)}, f32[4,8,8,17,32]{4,2,3,1,0:T(8,128)}) fusion(f32[4]{0:T(128)S(1)} %and_convert_fusion, pred[8,17]{0,1:T(8,128)(4,1)S(1)} %copy-done.14, f32[32]{0:T(128)S(1)} %copy-done.12, bf16[32,4,3,3,3]{0,1,4,3,2:T(4,128)(2,1)S(1)} %copy-done.11, bf16[4,6,8,1,7,2]{4,0,5,2,1,3:T(4,128)(2,1)S(1)} %slice.45, ...), kind=kOutput, calls=%fused_computation.37 | convolution fusion | flops 29002752 | bytes 900376 | tf_op jit(solution)/shard_map/conv_general_dilated | solution.py:29
  21.2 1.3 %fusion.54 = (bf16[4,8,1,8,16,32]{5,3,4,1,0,2:T(8,128)(2,1)S(1)}, bf16[4,8,1,8,16,32]{5,3,4,1,0,2:T(8,128)(2,1)}) fusion(bf16[4,8,1,8,17,32]{5,3,4,1,0,2:T(8,128)(2,1)S(1)} %bitcast.82), kind=kLoop, calls=%fused_computation.75 | loop fusion | bytes 1048576 | tf_op jit(solution)/shard_map/convert_element_type | solution.py:79
  22.7 2.8 %add_multiply_fusion = (f32[2,8,8,17,64]{4,2,3,1,0:T(8,128)S(1)}, bf16[2,8,8,17,64]{4,2,3,1,0:T(8,128)(2,1)}) fusion(f32[64]{0:T(128)S(1)} %copy-done.13, bf16[64,32,3,3,3]{0,1,4,3,2:T(8,128)(2,1)S(1)} %copy-done, bf16[4,8,1,8,1,32]{5,3,4,1,0,2:T(8,128)(2,1)S(1)} %pad.3, bf16[4,8,1,8,17,32]{5,3,4,1,0,2:T(8,128)(2,1)S(1)} %bitcast.83, ...), kind=kOutput, calls=%fused_computation.34 | convolution fusion | flops 222920704 | bytes 1257728 | tf_op jit(solution)/shard_map/conv_general_dilated | solution.py:29
  26.8 1.3 %collective-permute-start.3 = (bf16[1,64,1,8,128]{1,3,4,2,0:T(8,128)(2,1)}, bf16[1,64,1,8,128]{1,3,4,2,0:T(8,128)(2,1)}, u32[]{:S(2)}, u32[]{:S(2)}) collective-permute-start(bf16[1,64,1,8,128]{1,3,4,2,0:T(8,128)(2,1)} %get-tuple-element.34), channel_id=1, source_target_pairs={{1,0},{2,1},{3,2},{4,3},{5,4},{6,5},{7,6},{9,8},{10,9},{11,10},{12... | collective-permute-start | bytes 393224 | tf_op jit(solution)/shard_map/ppermute | solution.py:23
  28.1 5.6 %collective-permute-start.2 = (bf16[1,64,1,8,128]{1,3,4,2,0:T(8,128)(2,1)}, bf16[1,64,1,8,128]{1,3,4,2,0:T(8,128)(2,1)}, u32[]{:S(2)}, u32[]{:S(2)}) collective-permute-start(bf16[1,64,1,8,128]{1,3,4,2,0:T(8,128)(2,1)} %get-tuple-element.33), channel_id=1, source_target_pairs={{0,1},{1,2},{2,3},{3,4},{4,5},{5,6},{6,7},{8,9},{9,10},{10,11},{11... | collective-permute-start | bytes 393224 | tf_op jit(solution)/shard_map/ppermute | solution.py:22
  33.7 1.2 %copy.87 = bf16[4,6,8,1,7,1]{4,0,5,2,1,3:T(4,128)(2,1)S(1)} copy(bf16[4,6,8,1,7,1]{5,4,2,1,0,3:T(8,128)(2,1)S(1)} %copy-done.5) | data formatting | bytes 5376
  34.9 2.3 %copy.86 = bf16[4,6,8,1,8,16]{4,0,5,2,1,3:T(4,128)(2,1)} copy(bf16[4,6,8,1,8,16]{5,4,2,1,0,3:T(8,128)(2,1)} %get-tuple-element.36) | data formatting | bytes 98304
  37.2 2.2 %copy.85 = bf16[4,6,8,1,8,16]{4,0,5,2,1,3:T(4,128)(2,1)} copy(bf16[4,6,8,1,8,16]{5,4,2,1,0,3:T(8,128)(2,1)} %get-tuple-element.35) | data formatting | bytes 98304
  39.4 1.9 %copy.84 = bf16[4,6,8,1,7,1]{4,0,5,2,1,3:T(4,128)(2,1)} copy(bf16[4,6,8,1,7,1]{5,4,2,1,0,3:T(8,128)(2,1)S(1)} %copy-done.4) | data formatting | bytes 5376
  41.2 3.1 %copy.79 = bf16[4,6,8,8,17,1]{3,0,5,4,2,1:T(4,128)(2,1)} copy(bf16[4,6,8,8,17,1]{4,3,2,1,0,5:T(8,128)(2,1)} %reshape.94) | data formatting | bytes 104448 | tf_op jit(solution)/shard_map/concatenate | solution.py:24
  44.4 1.1 copy-done.1
  46.0 4.6 %fusion.19 = bf16[3,3,3,32,64,1]{4,3,2,5,1,0:T(8,128)(2,1)} fusion(bf16[64,2,8,8,17,1]{0,2,4,3,1,5:T(8,128)(2,1)S(1)} %bitcast.87, bf16[4,8,8,17,32,1]{4,2,3,1,0,5:T(8,128)(2,1)S(1)} %get-tuple-element.48, bf16[4,8,8,17,32,1]{4,2,3,1,0,5:T(8,128)(2,1)S(1)} %bitcast.84, bf16[4,8,8,17,32,1]{4,2,3,1,0,5:T(8,128)(2,1)S(1)} %get-tuple-element.47), kind=kOutput, calls=%fused_computation.29 | convolution fusion | flops 221485056 | bytes 1224704 | tf_op jit(solution)/shard_map/transpose | solution.py:93
  50.6 1.1 reshape.54
  51.7 0.9 fusion.33
  52.6 1.3 %maximum_bitcast_fusion.4 = bf16[64,4,8,1,128]{0,2,4,1,3:T(8,128)(2,1)S(1)} fusion(bf16[1,64,1,8,128]{1,3,4,2,0:T(8,128)(2,1)} %collective-permute-done.3, bf16[1,64,2,8,128]{1,3,4,2,0:T(8,128)(2,1)S(1)} %get-tuple-element.26, bf16[1,64,1,8,128]{1,3,4,2,0:T(8,128)(2,1)} %collective-permute-done.2), kind=kLoop, calls=%fused_computation.41 | loop fusion | flops 524288 | bytes 1048576 | tf_op jit(solution)/shard_map/concatenate | solution.py:24
  54.8 1.0 copy-done.16
  55.8 4.4 %select_reduce_fusion = (bf16[32]{0:T(256)(128)(2,1)S(1)}, bf16[2,8,8,17,32]{4,2,3,1,0:T(8,128)(2,1)S(1)}) fusion(pred[8,17]{0,1:T(8,128)(4,1)S(1)} %copy-done.15, f32[4,8,8,17,32]{4,2,3,1,0:T(8,128)S(1)} %copy-done.16, bf16[64,32,3,3,3]{0,1,4,3,2:T(8,128)(2,1)S(1)} %copy-done, bf16[64,4,8,1,7,2]{0,4,5,2,1,3:T(8,128)(2,1)S(1)} %slice.58, ...), kind=kOutput, calls=%fused_computation.33 | convolution fusion | flops 223367136 | bytes 1142984 | tf_op jit(solution)/shard_map/conv_general_dilated | solution.py:29
  60.2 4.0 %fusion.22 = bf16[3,3,3,4,32,1]{4,3,2,5,1,0:T(4,128)(2,1)S(1)} fusion(bf16[4,6,8,8,17,1]{3,0,5,4,2,1:T(4,128)(2,1)S(1)} %get-tuple-element.45, bf16[4,6,8,8,17,1]{3,0,5,4,2,1:T(4,128)(2,1)S(1)} %copy-done.6, bf16[4,6,8,8,17,1]{3,0,5,4,2,1:T(4,128)(2,1)S(1)} %get-tuple-element.46, bf16[2,8,8,17,32]{4,2,3,1,0:T(8,128)(2,1)S(1)} %get-tuple-element.44, ...), kind=kOutput, calls=%fused_computation.30 | convolution fusion | flops 14330240 | bytes 302984 | tf_op jit(solution)/shard_map/transpose | solution.py:94
  64.5 18.3 %all_to_all.15 = bf16[32,16,128]{2,1,0:T(8,128)(2,1)S(1)} all-to-all(bf16[32,16,128]{2,1,0:T(8,128)(2,1)S(1)} %bitcast.88), channel_id=1, replica_groups=mesh['z'=8,'x_hi'=2,'core'=2,'y'=4,'x_lo'=2] {'x_hi','core','y','x_lo'}, dimensions={0} | all-to-all | bytes 262144 | tf_op jit(solution)/shard_map/all_to_all | solution.py:56
  83.4 8.2 %all-to-all-start.1 = ((bf16[8,16,128]{2,1,0:T(8,128)(2,1)}), bf16[8,16,128]{2,1,0:T(8,128)(2,1)S(1)}, u32[]{:S(2)}, u32[]{:S(2)}) async-start(bf16[8,16,128]{2,1,0:T(8,128)(2,1)} %broadcast_in_dim.10), calls=%async_computation.1 | async-start | bytes 65536 | tf_op jit(solution)/shard_map/all_to_all | solution.py:56
  91.7 6.9 %all-to-all-done.1 = bf16[8,16,128]{2,1,0:T(8,128)(2,1)S(1)} async-done(((bf16[8,16,128]{2,1,0:T(8,128)(2,1)}), bf16[8,16,128]{2,1,0:T(8,128)(2,1)S(1)}, u32[]{:S(2)}, u32[]{:S(2)}) %all-to-all-start.1) | async-done | bytes 32800 | tf_op jit(solution)/shard_map/all_to_all | solution.py:56
  99.2 5.3 %all-to-all-start.2 = ((bf16[32,16,128]{2,1,0:T(8,128)(2,1)}), bf16[32,16,128]{2,1,0:T(8,128)(2,1)S(1)}, u32[]{:S(2)}, u32[]{:S(2)}) async-start(bf16[32,16,128]{2,1,0:T(8,128)(2,1)} %broadcast_in_dim.11), calls=%async_computation.2 | async-start | bytes 262144 | tf_op jit(solution)/shard_map/all_to_all | solution.py:56
  104.6 1.1 copy.83
  105.7 6.6 %all-to-all-done.2 = bf16[32,16,128]{2,1,0:T(8,128)(2,1)S(1)} async-done(((bf16[32,16,128]{2,1,0:T(8,128)(2,1)}), bf16[32,16,128]{2,1,0:T(8,128)(2,1)S(1)}, u32[]{:S(2)}, u32[]{:S(2)}) %all-to-all-start.2) | async-done | bytes 131104 | tf_op jit(solution)/shard_map/all_to_all | solution.py:56
  114.2 0.9 reshape.58
  (71 shorter events, 8.2 us)
Async XLA Ops:
  0.6 22.0 %copy-start = (bf16[64,32,3,3,3]{0,1,4,3,2:T(8,128)(2,1)S(1)}, bf16[64,32,3,3,3]{0,1,4,3,2:T(8,128)(2,1)}, u32[]{:S(2)}) copy-start(bf16[64,32,3,3,3]{0,1,4,3,2:T(8,128)(2,1)} %param.9) | copy-start | bytes 331780
  0.6 7.5 %collective-permute-start.1 = (bf16[1,4,2,8,128]{4,3,2,1,0:T(8,128)(2,1)}, bf16[1,4,2,8,128]{4,3,2,1,0:T(8,128)(2,1)S(1)}, u32[]{:S(2)}, u32[]{:S(2)}) collective-permute-start(bf16[1,4,2,8,128]{4,3,2,1,0:T(8,128)(2,1)} %param.6), channel_id=1, source_target_pairs={{1,0},{2,1},{3,2},{4,3},{5,4},{6,5},{7,6},{9,8},{10,9},{11,10},{12... | collective-permute-start | bytes 49160 | tf_op jit(solution)/shard_map/ppermute | solution.py:23
  2.1 6.1 %collective-permute-start = (bf16[1,4,2,8,128]{4,3,2,1,0:T(8,128)(2,1)}, bf16[1,4,2,8,128]{4,3,2,1,0:T(8,128)(2,1)S(1)}, u32[]{:S(2)}, u32[]{:S(2)}) collective-permute-start(bf16[1,4,2,8,128]{4,3,2,1,0:T(8,128)(2,1)} %param.6), channel_id=1, source_target_pairs={{0,1},{1,2},{2,3},{3,4},{4,5},{5,6},{6,7},{8,9},{9,10},{10,11},{11... | collective-permute-start | bytes 49160 | tf_op jit(solution)/shard_map/ppermute | solution.py:22
  11.4 2.9 %copy-start.11 = (bf16[32,4,3,3,3]{0,1,4,3,2:T(4,128)(2,1)S(1)}, bf16[32,4,3,3,3]{0,1,4,3,2:T(4,128)(2,1)}, u32[]{:S(2)}) copy-start(bf16[32,4,3,3,3]{0,1,4,3,2:T(4,128)(2,1)} %param.7) | copy-start | bytes 20740
  11.4 2.9 %copy-start.12 = (f32[32]{0:T(128)S(1)}, f32[32]{0:T(128)}, u32[]{:S(2)}) copy-start(f32[32]{0:T(128)} %param.8) | copy-start | bytes 388
  11.4 2.9 %copy-start.14 = (pred[8,17]{0,1:T(8,128)(4,1)S(1)}, pred[8,17]{0,1:T(8,128)(4,1)}, u32[]{:S(2)}) copy-start(pred[8,17]{0,1:T(8,128)(4,1)} %constant.56) | copy-start | bytes 412
  21.2 1.4 %copy-start.13 = (f32[64]{0:T(128)S(1)}, f32[64]{0:T(128)}, u32[]{:S(2)}) copy-start(f32[64]{0:T(128)} %param.10) | copy-start | bytes 772
  22.6 2.8 %copy-start.8 = (bf16[4,8,1,8,1,32]{5,3,4,1,0,2:T(8,128)(2,1)}, bf16[4,8,1,8,1,32]{5,3,4,1,0,2:T(8,128)(2,1)S(1)}, u32[]{:S(2)}) copy-start(bf16[4,8,1,8,1,32]{5,3,4,1,0,2:T(8,128)(2,1)S(1)} %pad.2) | copy-start | bytes 49156
  25.9 7.7 %copy-start.5 = (bf16[4,6,8,1,7,1]{5,4,2,1,0,3:T(8,128)(2,1)S(1)}, bf16[4,6,8,1,7,1]{5,4,2,1,0,3:T(8,128)(2,1)}, u32[]{:S(2)}) copy-start(bf16[4,6,8,1,7,1]{5,4,2,1,0,3:T(8,128)(2,1)} %get-tuple-element.38) | copy-start | bytes 8068
  26.8 25.9 %collective-permute-start.3 = (bf16[1,64,1,8,128]{1,3,4,2,0:T(8,128)(2,1)}, bf16[1,64,1,8,128]{1,3,4,2,0:T(8,128)(2,1)}, u32[]{:S(2)}, u32[]{:S(2)}) collective-permute-start(bf16[1,64,1,8,128]{1,3,4,2,0:T(8,128)(2,1)} %get-tuple-element.34), channel_id=1, source_target_pairs={{1,0},{2,1},{3,2},{4,3},{5,4},{6,5},{7,6},{9,8},{10,9},{11,10},{12... | collective-permute-start | bytes 393224 | tf_op jit(solution)/shard_map/ppermute | solution.py:23
  28.1 24.6 %collective-permute-start.2 = (bf16[1,64,1,8,128]{1,3,4,2,0:T(8,128)(2,1)}, bf16[1,64,1,8,128]{1,3,4,2,0:T(8,128)(2,1)}, u32[]{:S(2)}, u32[]{:S(2)}) collective-permute-start(bf16[1,64,1,8,128]{1,3,4,2,0:T(8,128)(2,1)} %get-tuple-element.33), channel_id=1, source_target_pairs={{0,1},{1,2},{2,3},{3,4},{4,5},{5,6},{6,7},{8,9},{9,10},{10,11},{11... | collective-permute-start | bytes 393224 | tf_op jit(solution)/shard_map/ppermute | solution.py:22
  34.9 4.5 %copy-start.4 = (bf16[4,6,8,1,7,1]{5,4,2,1,0,3:T(8,128)(2,1)S(1)}, bf16[4,6,8,1,7,1]{5,4,2,1,0,3:T(8,128)(2,1)}, u32[]{:S(2)}) copy-start(bf16[4,6,8,1,7,1]{5,4,2,1,0,3:T(8,128)(2,1)} %get-tuple-element.37) | copy-start | bytes 8068
  41.2 3.2 %copy-start.9 = (bf16[4,8,1,8,1,32]{5,3,4,1,0,2:T(8,128)(2,1)S(1)}, bf16[4,8,1,8,1,32]{5,3,4,1,0,2:T(8,128)(2,1)}, u32[]{:S(2)}) copy-start(bf16[4,8,1,8,1,32]{5,3,4,1,0,2:T(8,128)(2,1)} %copy-done.8) | copy-start | bytes 49156
  44.3 1.2 %copy-start.1 = (bf16[4,8,1,8,16,32]{5,3,4,1,0,2:T(8,128)(2,1)S(1)}, bf16[4,8,1,8,16,32]{5,3,4,1,0,2:T(8,128)(2,1)}, u32[]{:S(2)}) copy-start(bf16[4,8,1,8,16,32]{5,3,4,1,0,2:T(8,128)(2,1)} %get-tuple-element.28) | copy-start | bytes 786436
  46.0 5.7 %copy-start.2 = (bf16[4,6,8,1,8,16]{4,0,5,2,1,3:T(4,128)(2,1)S(1)}, bf16[4,6,8,1,8,16]{4,0,5,2,1,3:T(4,128)(2,1)}, u32[]{:S(2)}) copy-start(bf16[4,6,8,1,8,16]{4,0,5,2,1,3:T(4,128)(2,1)} %copy.86) | copy-start | bytes 147460
  46.0 5.7 %copy-start.3 = (bf16[4,6,8,1,8,16]{4,0,5,2,1,3:T(4,128)(2,1)S(1)}, bf16[4,6,8,1,8,16]{4,0,5,2,1,3:T(4,128)(2,1)}, u32[]{:S(2)}) copy-start(bf16[4,6,8,1,8,16]{4,0,5,2,1,3:T(4,128)(2,1)} %copy.85) | copy-start | bytes 147460
  46.0 5.7 %copy-start.10 = (bf16[4,6,8,1,7,1]{4,0,5,2,1,3:T(4,128)(2,1)S(1)}, bf16[4,6,8,1,7,1]{4,0,5,2,1,3:T(4,128)(2,1)}, u32[]{:S(2)}) copy-start(bf16[4,6,8,1,7,1]{4,0,5,2,1,3:T(4,128)(2,1)} %copy.84) | copy-start | bytes 8068
  54.1 0.7 copy-start.15
  54.2 1.6 %copy-start.16 = (f32[4,8,8,17,32]{4,2,3,1,0:T(8,128)S(1)}, f32[4,8,8,17,32]{4,2,3,1,0:T(8,128)}, u32[]{:S(2)}) copy-start(f32[4,8,8,17,32]{4,2,3,1,0:T(8,128)} %get-tuple-element.42) | copy-start | bytes 1671172
  55.8 4.4 %copy-start.6 = (bf16[4,6,8,8,17,1]{3,0,5,4,2,1:T(4,128)(2,1)S(1)}, bf16[4,6,8,8,17,1]{3,0,5,4,2,1:T(4,128)(2,1)}, u32[]{:S(2)}) copy-start(bf16[4,6,8,8,17,1]{3,0,5,4,2,1:T(4,128)(2,1)} %copy.79) | copy-start | bytes 156676
  60.2 31.4 %copy-start.7 = (bf16[2,8,8,17,64]{4,2,3,1,0:T(8,128)(2,1)S(1)}, bf16[2,8,8,17,64]{4,2,3,1,0:T(8,128)(2,1)}, u32[]{:S(2)}) copy-start(bf16[2,8,8,17,64]{4,2,3,1,0:T(8,128)(2,1)} %get-tuple-element.30) | copy-start | bytes 835588
  83.4 15.1 %all-to-all-start.1 = ((bf16[8,16,128]{2,1,0:T(8,128)(2,1)}), bf16[8,16,128]{2,1,0:T(8,128)(2,1)S(1)}, u32[]{:S(2)}, u32[]{:S(2)}) async-start(bf16[8,16,128]{2,1,0:T(8,128)(2,1)} %broadcast_in_dim.10), calls=%async_computation.1 | async-start | bytes 65536 | tf_op jit(solution)/shard_map/all_to_all | solution.py:56
  99.2 13.1 %all-to-all-start.2 = ((bf16[32,16,128]{2,1,0:T(8,128)(2,1)}), bf16[32,16,128]{2,1,0:T(8,128)(2,1)S(1)}, u32[]{:S(2)}, u32[]{:S(2)}) async-start(bf16[32,16,128]{2,1,0:T(8,128)(2,1)} %broadcast_in_dim.11), calls=%async_computation.2 | async-start | bytes 262144 | tf_op jit(solution)/shard_map/all_to_all | solution.py:56

commit v2 on v1

v2 whole, which is shorter than its diff:
```python
import jax
import jax.numpy as jnp
from jax import lax
from jax.experimental import pallas as pl
from jax.experimental.pallas import tpu as pltpu
from jax.sharding import Mesh
from jax.sharding import PartitionSpec as P

DP = ("z", "x_hi", "core")
DEPTH = ("y", "x_lo")
PLANE = ("x_hi", "core", "y", "x_lo")
LINE = "z"

BF = jnp.bfloat16
F32 = jnp.float32
HY = 8
HX = 128
CELLS = HY * HX
ROWS = HY + 1
C_IN = 4
C_ONE = 32
C_TWO = 64
V_PITCH = 72
C_PITCH = 40
F_PITCH = 24


def dot_nn(a, b):
    return lax.dot_general(a, b, (((1,), (0,)), ((), ())), preferred_element_type=F32)


def dot_nt(a, b):
    return lax.dot_general(a, b, (((1,), (1,)), ((), ())), preferred_element_type=F32)


def identity(n):
    return lax.broadcasted_iota(jnp.int32, (n, n), 0) == lax.broadcasted_iota(jnp.int32, (n, n), 1)


def column(row):
    n = row.shape[1]
    return jnp.sum(jnp.where(identity(n), jnp.broadcast_to(row, (n, n)), 0.0), axis=1, keepdims=True)


def transposed(w):
    return dot_nt(identity(w.shape[1]).astype(BF), w).astype(BF)


def sigmoid(v):
    return 1.0 / (1.0 + jnp.exp(-v))


def neighbours(x):
    lane = lax.broadcasted_iota(jnp.int32, x.shape, 1)
    before = jnp.where(lane == 0, 0.0, pltpu.roll(x, 1, 1))
    after = jnp.where(lane == HX - 1, 0.0, pltpu.roll(x, HX - 1, 1))
    return before, x, after


def compute(
    depth, vm2, vm1, v0, vp1, vp2, w1, b1, w2, b2, cm, c0, cp,
    features, packed,
    vs, x1, x1b, x3, s3, cs, fs, w1s, p1, pk,
):
    sources = ((vm2, 1), (vm1, 0), (vm1, 1), (v0, 0), (v0, 1), (vp1, 0), (vp1, 1), (vp2, 0))
    for p, (ref, z) in enumerate(sources):
        for i in range(C_IN):
            vs[i * V_PITCH + p * HY : i * V_PITCH + (p + 1) * HY, :] = ref[0, i, z].astype(F32)
    row_id = lax.broadcasted_iota(jnp.int32, (12, HX), 0)
    x1[36:48, :] = jnp.where(lax.broadcasted_iota(jnp.int32, (12, 8 * CELLS), 0) == 0, 1.0, 0.0)
    for p in range(8):
        x1[0:12, p * CELLS : p * CELLS + HX] = jnp.zeros((12, HX), F32)
        x1[24:36, p * CELLS + 7 * HX : (p + 1) * CELLS] = jnp.zeros((12, HX), F32)
        for y in range(HY):
            slab = vs[pl.ds(p * HY + y, C_IN, stride=V_PITCH), :]
            for c, moved in enumerate(neighbours(slab)):
                for b in range(3):
                    to = y + 1 - b
                    if 0 <= to < HY:
                        col = p * CELLS + to * HX
                        x1[b * 12 + c * 4 : b * 12 + c * 4 + 4, col : col + HX] = moved
        x1b[:, p * CELLS : (p + 1) * CELLS] = x1[:, p * CELLS : (p + 1) * CELLS].astype(BF)
    w1s[...] = jnp.zeros((144, C_ONE), F32)
    for a in range(3):
        for t in range(9):
            w1s[a * 48 + t * 4 : a * 48 + t * 4 + 4, :] = w1[a * 9 + t].astype(F32)
    w1t = [transposed(w1s[a * 48 : (a + 1) * 48, :].astype(BF)) for a in range(3)]
    bias1 = column(b1[...])
    bias2 = column(b2[...])
    for p in range(7):
        x3[:, p * ROWS * HX : p * ROWS * HX + HX] = jnp.zeros((96, HX), BF)
    for q in range(5):
        s3[:, q * ROWS * HX : q * ROWS * HX + HX] = jnp.zeros((192, HX), BF)
    first = depth[0] * 2 - 2
    for p in range(6):
        pre = bias1 + sum(dot_nn(w1t[a], x1b[:, (p + a) * CELLS : (p + a + 1) * CELLS]) for a in range(3))
        sig = sigmoid(pre)
        if p in (2, 3):
            p1[:, (p - 2) * CELLS : (p - 1) * CELLS] = sig * (1.0 + pre * (1.0 - sig))
        inside = jnp.logical_and(first + p >= 0, first + p < 16)
        act = pre * sig * jnp.where(inside, 1.0, 0.0)
        for y in range(HY):
            col = (1 + p * ROWS + y) * HX
            for c, moved in enumerate(neighbours(act[:, y * HX : (y + 1) * HX])):
                x3[c * C_ONE : (c + 1) * C_ONE, col : col + HX] = moved.astype(BF)
    for q, (ref, z) in enumerate(((cm, 0), (c0, 0), (c0, 1), (cp, 0))):
        for o in range(C_TWO):
            cs[o * C_PITCH + q * HY : o * C_PITCH + (q + 1) * HY, :] = ref[0, o, z].astype(F32)
    w2t = [transposed(w2[3 * k : 3 * k + 3].reshape(96, C_TWO)) for k in range(9)]
    for q in range(4):
        pre = bias2
        for k in range(9):
            col = ((q + k // 3) * ROWS + k % 3) * HX
            pre = pre + dot_nn(w2t[k], x3[:, col : col + CELLS])
        sig = sigmoid(pre)
        slope = sig * (1.0 + pre * (1.0 - sig))
        act = pre * sig
        for y in range(HY):
            cot = cs[pl.ds(q * HY + y, C_TWO, stride=C_PITCH), :]
            here = (cot * slope[:, y * HX : (y + 1) * HX]).astype(BF).astype(F32)
            col = (1 + q * ROWS + y) * HX
            for c, moved in enumerate(neighbours(here)):
                s3[c * C_TWO : (c + 1) * C_TWO, col : col + HX] = moved.astype(BF)
            if q in (1, 2):
                fs[pl.ds((q - 1) * HY + y, C_TWO, stride=F_PITCH), :] = act[:, y * HX : (y + 1) * HX]
    for o in range(C_TWO):
        for z in range(2):
            features[0, o, z] = fs[o * F_PITCH + z * HY : o * F_PITCH + (z + 1) * HY, :].astype(BF)
    mine = [s3[C_TWO : 2 * C_TWO, (1 + q * ROWS) * HX : (1 + q * ROWS) * HX + CELLS] for q in (1, 2)]
    pk[384:512, :] = jnp.zeros((128, HX), F32)
    for k in range(9):
        grad = 0.0
        for j in range(2):
            col = ((1 + j + k // 3) * ROWS + k % 3) * HX
            grad = grad + dot_nt(x3[:, col : col + CELLS], mine[j])
        pk[(k % 4) * 96 if k < 8 else 384 : (k % 4) * 96 + 96 if k < 8 else 480, (k // 4 % 2) * 64 : (k // 4 % 2) * 64 + 64] = grad
    ones = jnp.ones((8, CELLS), BF)
    bias_two = dot_nt(ones, mine[0]) + dot_nt(ones, mine[1])
    pk[480:488, 0:64] = bias_two
    flipped = []
    for k in range(9):
        flipped.append(jnp.concatenate([w2[(8 - k) * 3 + 2 - c] for c in range(3)], axis=1))
    ones_grad = []
    for j in range(2):
        back = 0.0
        for k in range(9):
            col = ((j + k // 3) * ROWS + k % 3) * HX
            back = back + dot_nn(flipped[k], s3[:, col : col + CELLS])
        slope1 = (back * p1[:, j * CELLS : (j + 1) * CELLS]).astype(BF)
        ones_grad.append([dot_nt(x1b[:, (2 + j + a) * CELLS : (3 + j + a) * CELLS], slope1) for a in range(3)])
    for a in range(3):
        grad = ones_grad[0][a] + ones_grad[1][a]
        pk[384 + a * 40 : 384 + a * 40 + 40, 64:96] = grad[:40]
    packed[...] = pk[...].astype(BF).reshape(32, 16, HX)


def unpack(total, two, one, bias_one, bias_two):
    flat = total[...].astype(F32).reshape(512, HX)
    for k in range(9):
        r = (k % 4) * 96 if k < 8 else 384
        lane = (k // 4 % 2) * 64
        two[3 * k : 3 * k + 3] = flat[r : r + 96, lane : lane + 64].reshape(3, C_ONE, C_TWO)
    for a in range(3):
        for t in range(9):
            r = 384 + a * 40 + t * 4
            one[a * 9 + t] = flat[r : r + 4, 64:96]
    bias_one[...] = flat[384 + 36 : 384 + 37, 64:96]
    bias_two[...] = flat[480:481, 0:64]


def exchange(x, axes):
    return lax.all_to_all(x, axes, 0, 0, tiled=True)


def reduced(x):
    plane = lax.axis_size(PLANE)
    line = lax.axis_size(LINE)
    part = exchange(x, PLANE)
    part = jnp.sum(part, axis=0, dtype=F32).astype(x.dtype)
    part = exchange(jnp.broadcast_to(part[None], (line,) + part.shape), LINE)
    part = jnp.sum(part, axis=0, dtype=F32).astype(x.dtype)
    return exchange(jnp.broadcast_to(part[None], (plane,) + part.shape), PLANE)


def shifted(x, step):
    size = lax.axis_size(DEPTH)
    pairs = [(i, i + step) for i in range(size) if 0 <= i + step < size]
    return lax.ppermute(x, DEPTH, pairs)


VMEM = pl.BlockSpec(memory_space=pltpu.VMEM)
SMEM = pl.BlockSpec(memory_space=pltpu.SMEM)


def local(depth, volumes, w1, b1, w2, b2, cots, interpret=False):
    return pl.pallas_call(
        compute,
        out_shape=(
            jax.ShapeDtypeStruct((1, C_TWO, 2, HY, HX), BF),
            jax.ShapeDtypeStruct((32, 16, HX), BF),
        ),
        in_specs=[SMEM] + [VMEM] * 12,
        out_specs=(VMEM, VMEM),
        scratch_shapes=[
            pltpu.VMEM((C_IN * V_PITCH, HX), F32),
            pltpu.VMEM((48, 8 * CELLS), F32),
            pltpu.VMEM((48, 8 * CELLS), BF),
            pltpu.VMEM((96, 55 * HX), BF),
            pltpu.VMEM((192, 37 * HX), BF),
            pltpu.VMEM((C_TWO * C_PITCH, HX), F32),
            pltpu.VMEM((C_TWO * F_PITCH, HX), F32),
            pltpu.VMEM((144, C_ONE), F32),
            pltpu.VMEM((C_ONE, 2 * CELLS), F32),
            pltpu.VMEM((512, HX), F32),
        ],
        compiler_params=pltpu.CompilerParams(vmem_limit_bytes=48 * 1024 * 1024),
        interpret=interpret,
        name="slab",
    )(depth, *volumes, w1, b1, w2, b2, *cots)


def split(total, interpret=False):
    return pl.pallas_call(
        unpack,
        out_shape=(
            jax.ShapeDtypeStruct((27, C_ONE, C_TWO), F32),
            jax.ShapeDtypeStruct((27, C_IN, C_ONE), F32),
            jax.ShapeDtypeStruct((1, C_ONE), F32),
            jax.ShapeDtypeStruct((1, C_TWO), F32),
        ),
        in_specs=[VMEM],
        out_specs=(VMEM,) * 4,
        interpret=interpret,
        name="unpack",
    )(total)


def per_device(volume, kernel_one, bias_one, kernel_two, bias_two, cotangent):
    volumes = (shifted(volume, 2), shifted(volume, 1), volume, shifted(volume, -1), shifted(volume, -2))
    cots = (shifted(cotangent[:, :, 1:], 1), cotangent, shifted(cotangent[:, :, :1], -1))
    depth = lax.axis_index(DEPTH).astype(jnp.int32).reshape(1)
    w1 = jnp.transpose(kernel_one, (2, 3, 4, 1, 0)).reshape(27, C_IN, C_ONE)
    w2 = jnp.transpose(kernel_two, (2, 3, 4, 1, 0)).reshape(27, C_ONE, C_TWO)
    features, packed = local(depth, volumes, w1, bias_one[None], w2, bias_two[None], cots)
    two, one, b1, b2 = split(reduced(packed))
    two = jnp.transpose(two.reshape(3, 3, 3, C_ONE, C_TWO), (4, 3, 0, 1, 2))
    one = jnp.transpose(one.reshape(3, 3, 3, C_IN, C_ONE), (4, 3, 0, 1, 2))
    return (features, one, b1[0], two, b2[0])


def solution(mesh):
    cut = Mesh(mesh.devices.reshape(8, 2, 2, 4, 2), DP + DEPTH)
    return jax.shard_map(
        per_device,
        mesh=cut,
        in_specs=(
            P(DP, None, DEPTH, None, None),
            P(),
            P(),
            P(),
            P(),
            P(DP, None, DEPTH, None, None),
        ),
        out_specs=(P(DP, None, DEPTH, None, None), P(), P(), P(), P()),
        check_vma=False,
    )
```

time: 116 us -> 74.3 us (0.64)
  local copies, waits for them, and re-layouts: 29.5 us -> 1.72 us
  blocking collectives: 18.3 us -> 45 us
  matrix products: 22.5 us -> 0 us
  waiting for transfers between devices: 13.5 us -> 3.17 us
  starting transfers between devices: 26.3 us -> 16.5 us
  Pallas kernels: 0 us -> 6.61 us
  other arithmetic: 3.97 us -> 0.05 us
    all_to_all x1 -> x3, blocking collectives: 18.3 us -> 45 us  [exchange(): return lax.all_to_all(x, axes, 0, 0, tiled=True)]
    conv_general_dilated x3 -> x0, matrix products: 13.9 us -> none  [convolve(): lax.conv_general_dilated(inputs, kernel, (1, 1, 1), ((depth_pad, depth_pa...]
    all_to_all x2 -> x0, waiting for transfers between devices: 13.5 us -> none  [exchange(): return lax.all_to_all(x, axes, 0, 0, tiled=True)]
    all_to_all x2 -> x0, starting transfers between devices: 13.5 us -> none  [exchange(): return lax.all_to_all(x, axes, 0, 0, tiled=True)]
    unnamed x40 -> x12, local copies, waits for them, and re-layouts: 12.7 us -> 0.65 us
    transpose x2 -> x0, matrix products: 8.56 us -> none  [the longest x1 4.57 us: per_device(): two = jnp.transpose(grad_two, (2, 3, 4, 1, 0)).reshape(432, 128)]
    concatenate x8 -> x0, local copies, waits for them, and re-layouts: 6.92 us -> none  [the longest x7 6.84 us: extended(): x = jnp.concatenate([before, x, after], axis=dim)]
    pallas_call x0 -> x2, Pallas kernels: none -> 6.61 us  [the longest x1 4.82 us: local(): pl.pallas_call(compute, out_shape=(jax.ShapeDtypeStruct((1, C_TWO, 2, HY,...]
  transfers between devices with their start and end apart: 6 -> 6, of which waited for: 2 -> 1; matrix products, arithmetic and copies ran while one was open for 18% -> 0% of each run, Pallas kernels for 0% -> 0%
where the time goes in v2:
time: 74.3 us; the launch traced here: 73.9 us
  blocking collectives  45 us (61%)
  starting transfers between devices  16.5 us (22%)
  Pallas kernels  6.61 us (9%)
  waiting for transfers between devices  3.17 us (4%)
  local copies, waits for them, and re-layouts  1.72 us (2%)
  between operations  0.82 us (1%)
    all_to_all x3, blocking collectives, exchange(): return lax.all_to_all(x, axes, 0, 0, tiled=True)  45 us
    ppermute x6, starting transfers between devices, shifted(): return lax.ppermute(x, DEPTH, pairs)  16.5 us
    pallas_call x1, Pallas kernels, local(): pl.pallas_call(compute, out_shape=(jax.ShapeDtypeStruct((1, C_TWO, 2, HY,...  4.82 us
    ppermute x6, waiting for transfers between devices, shifted(): return lax.ppermute(x, DEPTH, pairs)  3.17 us
    pallas_call x1, Pallas kernels, split(): pl.pallas_call(unpack, out_shape=(jax.ShapeDtypeStruct((27, C_ONE, C_TWO)...  1.79 us
  transfers between devices with their start and end apart: 6, of which 1 were waited for; matrix products, arithmetic and copies ran while one was open for 0% of the time, Pallas kernels for 0%

profile of v2, /device:TPU:1, one launch (start us, length us, event | category | flops | bytes accessed | tf_op | source)
XLA Modules:
  0.0 73.9 jit_solution(16200659388947555213)
XLA Ops:
  0.6 0.0 copy-start
  0.6 0.0 copy-start.3
  0.7 0.0 copy-start.1
  0.7 1.0 %fusion = (bf16[1,64,1,8,128]{4,3,2,1,0:T(8,128)(2,1)S(1)}, bf16[1,64,1,8,128]{4,3,2,1,0:T(8,128)(2,1)S(1)}) fusion(bf16[1,64,2,8,128]{4,3,2,1,0:T(8,128)(2,1)} %c0.1), kind=kLoop, calls=%fused_computation | loop fusion | bytes 524288 | tf_op jit(solution)/shard_map/slice | solution.py:240
  1.7 0.0 copy-start.2
  1.7 1.3 %collective-permute-start.5 = (bf16[1,64,1,8,128]{4,3,2,1,0:T(8,128)(2,1)S(1)}, bf16[1,64,1,8,128]{4,3,2,1,0:T(8,128)(2,1)S(1)}, u32[]{:S(2)}, u32[]{:S(2)}) collective-permute-start(bf16[1,64,1,8,128]{4,3,2,1,0:T(8,128)(2,1)S(1)} %get-tuple-element.17), channel_id=1, source_target_pairs={{1,0},{2,1},{3,2},{4,3},{5,4},{6,5},{7,6},{9,8},{10,9},{11,10},{12... | collective-permute-start | bytes 393224 | tf_op jit(solution)/shard_map/ppermute | solution.py:188
  3.0 4.6 %collective-permute-start.4 = (bf16[1,64,1,8,128]{4,3,2,1,0:T(8,128)(2,1)S(1)}, bf16[1,64,1,8,128]{4,3,2,1,0:T(8,128)(2,1)S(1)}, u32[]{:S(2)}, u32[]{:S(2)}) collective-permute-start(bf16[1,64,1,8,128]{4,3,2,1,0:T(8,128)(2,1)S(1)} %get-tuple-element.18), channel_id=1, source_target_pairs={{0,1},{1,2},{2,3},{3,4},{4,5},{5,6},{6,7},{8,9},{9,10},{10,11},{11... | collective-permute-start | bytes 393224 | tf_op jit(solution)/shard_map/ppermute | solution.py:188
  7.6 0.0 copy-done.3
  7.6 1.3 %collective-permute-start.2 = (bf16[1,4,2,8,128]{4,3,2,1,0:T(8,128)(2,1)S(1)}, bf16[1,4,2,8,128]{4,3,2,1,0:T(8,128)(2,1)S(1)}, u32[]{:S(2)}, u32[]{:S(2)}) collective-permute-start(bf16[1,4,2,8,128]{4,3,2,1,0:T(8,128)(2,1)S(1)} %copy-done.3), channel_id=1, source_target_pairs={{1,0},{2,1},{3,2},{4,3},{5,4},{6,5},{7,6},{9,8},{10,9},{11,10},{12... | collective-permute-start | bytes 49160 | tf_op jit(solution)/shard_map/ppermute | solution.py:188
  8.9 4.9 %collective-permute-start.1 = (bf16[1,4,2,8,128]{4,3,2,1,0:T(8,128)(2,1)S(1)}, bf16[1,4,2,8,128]{4,3,2,1,0:T(8,128)(2,1)S(1)}, u32[]{:S(2)}, u32[]{:S(2)}) collective-permute-start(bf16[1,4,2,8,128]{4,3,2,1,0:T(8,128)(2,1)S(1)} %copy-done.3), channel_id=1, source_target_pairs={{0,1},{1,2},{2,3},{3,4},{4,5},{5,6},{6,7},{8,9},{9,10},{10,11},{11... | collective-permute-start | bytes 49160 | tf_op jit(solution)/shard_map/ppermute | solution.py:188
  13.8 3.2 %collective-permute-start = (bf16[1,4,2,8,128]{4,3,2,1,0:T(8,128)(2,1)S(1)}, bf16[1,4,2,8,128]{4,3,2,1,0:T(8,128)(2,1)S(1)}, u32[]{:S(2)}, u32[]{:S(2)}) collective-permute-start(bf16[1,4,2,8,128]{4,3,2,1,0:T(8,128)(2,1)S(1)} %copy-done.3), channel_id=1, source_target_pairs={{0,2},{1,3},{2,4},{3,5},{4,6},{5,7},{8,10},{9,11},{10,12},{11,13},... | collective-permute-start | bytes 49160 | tf_op jit(solution)/shard_map/ppermute | solution.py:188
  17.0 0.0 collective-permute-done.2.vp1
  17.0 1.3 %collective-permute-start.3 = (bf16[1,4,2,8,128]{4,3,2,1,0:T(8,128)(2,1)S(1)}, bf16[1,4,2,8,128]{4,3,2,1,0:T(8,128)(2,1)S(1)}, u32[]{:S(2)}, u32[]{:S(2)}) collective-permute-start(bf16[1,4,2,8,128]{4,3,2,1,0:T(8,128)(2,1)S(1)} %copy-done.3), channel_id=1, source_target_pairs={{2,0},{3,1},{4,2},{5,3},{6,4},{7,5},{10,8},{11,9},{12,10},{13,11},... | collective-permute-start | bytes 49160 | tf_op jit(solution)/shard_map/ppermute | solution.py:188
  18.3 0.0 collective-permute-done.1.vm1
  18.3 0.0 collective-permute-done.vm2
  18.3 3.2 %collective-permute-done.3.vp2 = bf16[1,4,2,8,128]{4,3,2,1,0:T(8,128)(2,1)S(1)} collective-permute-done((bf16[1,4,2,8,128]{4,3,2,1,0:T(8,128)(2,1)S(1)}, bf16[1,4,2,8,128]{4,3,2,1,0:T(8,128)(2,1)S(1)}, u32[]{:S(2)}, u32[]{:S(2)}) %collective-permute-start.3) | collective-permute-done | bytes 16416 | tf_op jit(solution)/shard_map/ppermute | solution.py:188
  21.5 0.0 collective-permute-done.5.cp
  21.5 0.0 collective-permute-done.4.cm
  21.5 0.0 copy-start.4
  21.5 0.0 copy-start.5
  21.5 0.0 copy-done
  21.5 0.0 copy-done.1
  21.5 0.0 copy-done.2
  21.6 0.6 copy-done.4
  22.2 0.0 copy-done.5
  22.2 4.8 %slab.1 = (bf16[1,64,2,8,128]{4,3,2,1,0:T(8,128)(2,1)}, bf16[32,16,128]{2,1,0:T(8,128)(2,1)S(1)}) custom-call(s32[1]{0:T(128)} %bitcast.depth, bf16[1,4,2,8,128]{4,3,2,1,0:T(8,128)(2,1)S(1)} %collective-permute-done.vm2, bf16[1,4,2,8,128]{4,3,2,1,0:T(8,128)(2,1)S(1)} %collective-permute-done.1.vm1, bf16[1,4,2,8,128]{4,3,2,1,0:T(8,128)(2,1)S(1)} %copy-done.3, ...), custom_call_target="tpu_custom_call" | custom-call | tf_op jit(solution)/shard_map/slab/pallas_call | solution.py:196
  27.0 17.1 %all_to_all.15 = bf16[32,16,128]{2,1,0:T(8,128)(2,1)S(1)} all-to-all(bf16[32,16,128]{2,1,0:T(8,128)(2,1)S(1)} %get-tuple-element.12), channel_id=1, replica_groups=mesh['z'=8,'x_hi'=2,'core'=2,'y'=4,'x_lo'=2] {'x_hi','core','y','x_lo'}, dimensions={0} | all-to-all | bytes 262144 | tf_op jit(solution)/shard_map/all_to_all | solution.py:172
  44.2 15.0 %all_to_all.16 = bf16[8,16,128]{2,1,0:T(8,128)(2,1)S(1)} all-to-all(bf16[8,16,128]{2,1,0:T(8,128)(2,1)S(1)} %broadcast_in_dim.20), channel_id=1, replica_groups=mesh['z'=8,'x_hi'=2,'core'=2,'y'=4,'x_lo'=2] {'z'}, dimensions={0} | all-to-all | bytes 65536 | tf_op jit(solution)/shard_map/all_to_all | solution.py:172
  59.2 12.9 %all_to_all.17.total = bf16[32,16,128]{2,1,0:T(8,128)(2,1)} all-to-all(bf16[32,16,128]{2,1,0:T(8,128)(2,1)S(1)} %broadcast_in_dim.21), channel_id=1, replica_groups=mesh['z'=8,'x_hi'=2,'core'=2,'y'=4,'x_lo'=2] {'x_hi','core','y','x_lo'}, dimensions={0} | all-to-all | bytes 262144 | tf_op jit(solution)/shard_map/all_to_all | solution.py:172
  72.1 1.8 %unpack.1 = (f32[27,32,64]{2,1,0:T(8,128)}, f32[27,4,32]{2,1,0:T(4,128)}, f32[1,32]{1,0:T(1,128)}, f32[1,64]{1,0:T(1,128)}) custom-call(bf16[32,16,128]{2,1,0:T(8,128)(2,1)} %all_to_all.17.total), custom_call_target="tpu_custom_call" | custom-call | tf_op jit(solution)/shard_map/unpack/pallas_call | solution.py:223
  (4 shorter events, 0.1 us)
Async XLA Ops:
  0.6 20.9 %copy-start = (bf16[1,64,2,8,128]{4,3,2,1,0:T(8,128)(2,1)S(1)}, bf16[1,64,2,8,128]{4,3,2,1,0:T(8,128)(2,1)}, u32[]{:S(2)}) copy-start(bf16[1,64,2,8,128]{4,3,2,1,0:T(8,128)(2,1)} %c0.1) | copy-start | bytes 786436
  0.6 7.0 %copy-start.3 = (bf16[1,4,2,8,128]{4,3,2,1,0:T(8,128)(2,1)S(1)}, bf16[1,4,2,8,128]{4,3,2,1,0:T(8,128)(2,1)}, u32[]{:S(2)}) copy-start(bf16[1,4,2,8,128]{4,3,2,1,0:T(8,128)(2,1)} %v0.1) | copy-start | bytes 49156
  0.7 20.9 %copy-start.1 = (bf16[64,32,3,3,3]{0,1,4,3,2:T(8,128)(2,1)S(1)}, bf16[64,32,3,3,3]{0,1,4,3,2:T(8,128)(2,1)}, u32[]{:S(2)}) copy-start(bf16[64,32,3,3,3]{0,1,4,3,2:T(8,128)(2,1)} %param.9) | copy-start | bytes 331780
  1.7 19.8 %copy-start.2 = (bf16[32,4,3,3,3]{0,1,4,3,2:T(4,128)(2,1)S(1)}, bf16[32,4,3,3,3]{0,1,4,3,2:T(4,128)(2,1)}, u32[]{:S(2)}) copy-start(bf16[32,4,3,3,3]{0,1,4,3,2:T(4,128)(2,1)} %param.7) | copy-start | bytes 20740
  1.7 19.8 %collective-permute-start.5 = (bf16[1,64,1,8,128]{4,3,2,1,0:T(8,128)(2,1)S(1)}, bf16[1,64,1,8,128]{4,3,2,1,0:T(8,128)(2,1)S(1)}, u32[]{:S(2)}, u32[]{:S(2)}) collective-permute-start(bf16[1,64,1,8,128]{4,3,2,1,0:T(8,128)(2,1)S(1)} %get-tuple-element.17), channel_id=1, source_target_pairs={{1,0},{2,1},{3,2},{4,3},{5,4},{6,5},{7,6},{9,8},{10,9},{11,10},{12... | collective-permute-start | bytes 393224 | tf_op jit(solution)/shard_map/ppermute | solution.py:188
  3.0 18.5 %collective-permute-start.4 = (bf16[1,64,1,8,128]{4,3,2,1,0:T(8,128)(2,1)S(1)}, bf16[1,64,1,8,128]{4,3,2,1,0:T(8,128)(2,1)S(1)}, u32[]{:S(2)}, u32[]{:S(2)}) collective-permute-start(bf16[1,64,1,8,128]{4,3,2,1,0:T(8,128)(2,1)S(1)} %get-tuple-element.18), channel_id=1, source_target_pairs={{0,1},{1,2},{2,3},{3,4},{4,5},{5,6},{6,7},{8,9},{9,10},{10,11},{11... | collective-permute-start | bytes 393224 | tf_op jit(solution)/shard_map/ppermute | solution.py:188
  7.6 9.4 %collective-permute-start.2 = (bf16[1,4,2,8,128]{4,3,2,1,0:T(8,128)(2,1)S(1)}, bf16[1,4,2,8,128]{4,3,2,1,0:T(8,128)(2,1)S(1)}, u32[]{:S(2)}, u32[]{:S(2)}) collective-permute-start(bf16[1,4,2,8,128]{4,3,2,1,0:T(8,128)(2,1)S(1)} %copy-done.3), channel_id=1, source_target_pairs={{1,0},{2,1},{3,2},{4,3},{5,4},{6,5},{7,6},{9,8},{10,9},{11,10},{12... | collective-permute-start | bytes 49160 | tf_op jit(solution)/shard_map/ppermute | solution.py:188
  8.9 9.4 %collective-permute-start.1 = (bf16[1,4,2,8,128]{4,3,2,1,0:T(8,128)(2,1)S(1)}, bf16[1,4,2,8,128]{4,3,2,1,0:T(8,128)(2,1)S(1)}, u32[]{:S(2)}, u32[]{:S(2)}) collective-permute-start(bf16[1,4,2,8,128]{4,3,2,1,0:T(8,128)(2,1)S(1)} %copy-done.3), channel_id=1, source_target_pairs={{0,1},{1,2},{2,3},{3,4},{4,5},{5,6},{6,7},{8,9},{9,10},{10,11},{11... | collective-permute-start | bytes 49160 | tf_op jit(solution)/shard_map/ppermute | solution.py:188
  13.8 4.5 %collective-permute-start = (bf16[1,4,2,8,128]{4,3,2,1,0:T(8,128)(2,1)S(1)}, bf16[1,4,2,8,128]{4,3,2,1,0:T(8,128)(2,1)S(1)}, u32[]{:S(2)}, u32[]{:S(2)}) collective-permute-start(bf16[1,4,2,8,128]{4,3,2,1,0:T(8,128)(2,1)S(1)} %copy-done.3), channel_id=1, source_target_pairs={{0,2},{1,3},{2,4},{3,5},{4,6},{5,7},{8,10},{9,11},{10,12},{11,13},... | collective-permute-start | bytes 49160 | tf_op jit(solution)/shard_map/ppermute | solution.py:188
  17.0 4.5 %collective-permute-start.3 = (bf16[1,4,2,8,128]{4,3,2,1,0:T(8,128)(2,1)S(1)}, bf16[1,4,2,8,128]{4,3,2,1,0:T(8,128)(2,1)S(1)}, u32[]{:S(2)}, u32[]{:S(2)}) collective-permute-start(bf16[1,4,2,8,128]{4,3,2,1,0:T(8,128)(2,1)S(1)} %copy-done.3), channel_id=1, source_target_pairs={{2,0},{3,1},{4,2},{5,3},{6,4},{7,5},{10,8},{11,9},{12,10},{13,11},... | collective-permute-start | bytes 49160 | tf_op jit(solution)/shard_map/ppermute | solution.py:188
  21.5 0.7 copy-start.4
  21.5 0.7 copy-start.5

commit v3 on v2

v3 whole, which is shorter than its diff:
```python
import jax
import jax.numpy as jnp
from jax import lax
from jax.experimental import pallas as pl
from jax.experimental.pallas import tpu as pltpu
from jax.sharding import Mesh
from jax.sharding import PartitionSpec as P

DP = ("z", "x_hi", "core")
DEPTH = ("y", "x_lo")
PLANE = ("x_hi", "core", "y", "x_lo")
LINE = "z"

BF = jnp.bfloat16
F32 = jnp.float32
HY = 8
HX = 128
CELLS = HY * HX
ROWS = HY + 1
C_IN = 4
C_ONE = 32
C_TWO = 64
V_PITCH = 56
C_PITCH = 24


def dot_nn(a, b):
    return lax.dot_general(a, b, (((1,), (0,)), ((), ())), preferred_element_type=F32)


def dot_nt(a, b):
    return lax.dot_general(a, b, (((1,), (1,)), ((), ())), preferred_element_type=F32)


def identity(n):
    return lax.broadcasted_iota(jnp.int32, (n, n), 0) == lax.broadcasted_iota(jnp.int32, (n, n), 1)


def column(row):
    n = row.shape[1]
    return jnp.sum(jnp.where(identity(n), jnp.broadcast_to(row, (n, n)), 0.0), axis=1, keepdims=True)


def transposed(w):
    return dot_nt(identity(w.shape[1]).astype(BF), w).astype(BF)


def sigmoid(v):
    return 1.0 / (1.0 + jnp.exp(-v))


def neighbours(x):
    lane = lax.broadcasted_iota(jnp.int32, x.shape, 1)
    before = jnp.where(lane == 0, 0.0, pltpu.roll(x, 1, 1))
    after = jnp.where(lane == HX - 1, 0.0, pltpu.roll(x, HX - 1, 1))
    return before, x, after


def compute(
    depth, va, v0, vb, w1, b1, w2, b2, c0,
    features, packed,
    vs, x1, x1b, x3, s3, cs, fs, w1s, p1, pk,
):
    even = depth[0] % 2 == 0
    for p in range(6):
        for i in range(C_IN):
            if p in (2, 3):
                plane = v0[0, i, p % 2].astype(F32)
            else:
                near = va[0, i, p % 2].astype(F32)
                far = vb[0, i, p % 2].astype(F32)
                plane = jnp.where(even, far, near) if p < 2 else jnp.where(even, near, far)
            vs[i * V_PITCH + p * HY : i * V_PITCH + (p + 1) * HY, :] = plane
    x1[36:48, :] = jnp.where(lax.broadcasted_iota(jnp.int32, (12, 6 * CELLS), 0) == 0, 1.0, 0.0)
    for p in range(6):
        x1[0:12, p * CELLS : p * CELLS + HX] = jnp.zeros((12, HX), F32)
        x1[24:36, p * CELLS + 7 * HX : (p + 1) * CELLS] = jnp.zeros((12, HX), F32)
        for y in range(HY):
            slab = vs[pl.ds(p * HY + y, C_IN, stride=V_PITCH), :]
            for c, moved in enumerate(neighbours(slab)):
                for b in range(3):
                    to = y + 1 - b
                    if 0 <= to < HY:
                        col = p * CELLS + to * HX
                        x1[b * 12 + c * 4 : b * 12 + c * 4 + 4, col : col + HX] = moved
        x1b[:, p * CELLS : (p + 1) * CELLS] = x1[:, p * CELLS : (p + 1) * CELLS].astype(BF)
    w1s[...] = jnp.zeros((144, C_ONE), F32)
    for a in range(3):
        for t in range(9):
            w1s[a * 48 + t * 4 : a * 48 + t * 4 + 4, :] = w1[a * 9 + t].astype(F32)
    w1t = [transposed(w1s[a * 48 : (a + 1) * 48, :].astype(BF)) for a in range(3)]
    bias1 = column(b1[...])
    bias2 = column(b2[...])
    for p in range(5):
        x3[:, p * ROWS * HX : p * ROWS * HX + HX] = jnp.zeros((96, HX), BF)
    for q in range(3):
        s3[:, q * ROWS * HX : q * ROWS * HX + HX] = jnp.zeros((192, HX), BF)
    for p in range(4):
        pre = bias1 + sum(dot_nn(w1t[a], x1b[:, (p + a) * CELLS : (p + a + 1) * CELLS]) for a in range(3))
        sig = sigmoid(pre)
        slope = sig * (1.0 + pre * (1.0 - sig))
        act = pre * sig
        if p in (0, 3):
            inside = jnp.where(depth[0] > 0 if p == 0 else depth[0] < depth[1] - 1, 1.0, 0.0)
            slope = slope * inside
            act = act * inside
        p1[:, p * CELLS : (p + 1) * CELLS] = slope
        for y in range(HY):
            col = (1 + p * ROWS + y) * HX
            for c, moved in enumerate(neighbours(act[:, y * HX : (y + 1) * HX])):
                x3[c * C_ONE : (c + 1) * C_ONE, col : col + HX] = moved.astype(BF)
    for z in range(2):
        for o in range(C_TWO):
            cs[o * C_PITCH + z * HY : o * C_PITCH + (z + 1) * HY, :] = c0[0, o, z].astype(F32)
    w2t = [transposed(w2[3 * k : 3 * k + 3].reshape(96, C_TWO)) for k in range(9)]
    for q in range(2):
        pre = bias2
        for k in range(9):
            col = ((q + k // 3) * ROWS + k % 3) * HX
            pre = pre + dot_nn(w2t[k], x3[:, col : col + CELLS])
        sig = sigmoid(pre)
        slope = sig * (1.0 + pre * (1.0 - sig))
        act = pre * sig
        for y in range(HY):
            row = q * HY + y
            cot = cs[pl.ds(row, C_TWO, stride=C_PITCH), :]
            here = (cot * slope[:, y * HX : (y + 1) * HX]).astype(BF).astype(F32)
            col = (1 + q * ROWS + y) * HX
            for c, moved in enumerate(neighbours(here)):
                s3[c * C_TWO : (c + 1) * C_TWO, col : col + HX] = moved.astype(BF)
            fs[pl.ds(row, C_TWO, stride=C_PITCH), :] = act[:, y * HX : (y + 1) * HX]
    for o in range(C_TWO):
        for z in range(2):
            features[0, o, z] = fs[o * C_PITCH + z * HY : o * C_PITCH + (z + 1) * HY, :].astype(BF)
    mine = [s3[C_TWO : 2 * C_TWO, (1 + q * ROWS) * HX : (1 + q * ROWS) * HX + CELLS] for q in range(2)]
    pk[384:512, :] = jnp.zeros((128, HX), F32)
    for k in range(9):
        grad = 0.0
        for j in range(2):
            col = ((j + k // 3) * ROWS + k % 3) * HX
            grad = grad + dot_nt(x3[:, col : col + CELLS], mine[j])
        row, lane = place(k)
        pk[row : row + 96, lane : lane + C_TWO] = grad
    ones = jnp.ones((8, CELLS), BF)
    pk[480:488, 0:C_TWO] = dot_nt(ones, mine[0]) + dot_nt(ones, mine[1])
    flipped = []
    for k in range(9):
        flipped.append(jnp.concatenate([w2[(8 - k) * 3 + 2 - c] for c in range(3)], axis=1))
    grads = [0.0, 0.0, 0.0]
    for t in range(4):
        back = 0.0
        for k in range(9):
            j = t + k // 3 - 2
            if 0 <= j < 2:
                col = (j * ROWS + k % 3) * HX
                back = back + dot_nn(flipped[k], s3[:, col : col + CELLS])
        share = back * p1[:, t * CELLS : (t + 1) * CELLS]
        high = share.astype(BF)
        share = jnp.concatenate([high, (share - high.astype(F32)).astype(BF)], axis=0)
        for a in range(3):
            grads[a] = grads[a] + dot_nt(x1b[:, (t + a) * CELLS : (t + a + 1) * CELLS], share)
    for a in range(3):
        grad = grads[a][:40]
        pk[384 + a * 40 : 384 + a * 40 + 40, C_TWO : C_TWO + C_ONE] = grad[:, :C_ONE] + grad[:, C_ONE:]
    packed[...] = pk[...].astype(BF).reshape(32, 16, HX)


def place(k):
    return ((k % 4) * 96, (k // 4) * C_TWO) if k < 8 else (384, 0)


def unpack(total, two, one, bias_one, bias_two):
    flat = total[...].astype(F32).reshape(512, HX)
    for k in range(9):
        r, lane = place(k)
        two[3 * k : 3 * k + 3] = flat[r : r + 96, lane : lane + 64].reshape(3, C_ONE, C_TWO)
    for a in range(3):
        for t in range(9):
            r = 384 + a * 40 + t * 4
            one[a * 9 + t] = flat[r : r + 4, 64:96]
    bias_one[...] = flat[384 + 36 : 384 + 37, 64:96]
    bias_two[...] = flat[480:481, 0:64]


def exchange(x, axes):
    return lax.all_to_all(x, axes, 0, 0, tiled=True)


def reduced(x):
    plane = lax.axis_size(PLANE)
    line = lax.axis_size(LINE)
    part = exchange(x, PLANE)
    part = jnp.sum(part, axis=0, dtype=F32).astype(x.dtype)
    part = exchange(jnp.broadcast_to(part[None], (line,) + part.shape), LINE)
    part = jnp.sum(part, axis=0, dtype=F32).astype(x.dtype)
    return exchange(jnp.broadcast_to(part[None], (plane,) + part.shape), PLANE)


def swapped(x, first):
    size = lax.axis_size(DEPTH)
    ups = [(i, i + 1) for i in range(first, size - 1, 2)]
    return lax.ppermute(x, DEPTH, ups + [(j, i) for i, j in ups])


VMEM = pl.BlockSpec(memory_space=pltpu.VMEM)
SMEM = pl.BlockSpec(memory_space=pltpu.SMEM)


def local(depth, volumes, w1, b1, w2, b2, cot, interpret=False):
    return pl.pallas_call(
        compute,
        out_shape=(
            jax.ShapeDtypeStruct((1, C_TWO, 2, HY, HX), BF),
            jax.ShapeDtypeStruct((32, 16, HX), BF),
        ),
        in_specs=[SMEM] + [VMEM] * 8,
        out_specs=(VMEM, VMEM),
        scratch_shapes=[
            pltpu.VMEM((C_IN * V_PITCH, HX), F32),
            pltpu.VMEM((48, 6 * CELLS), F32),
            pltpu.VMEM((48, 6 * CELLS), BF),
            pltpu.VMEM((96, 37 * HX), BF),
            pltpu.VMEM((192, 19 * HX), BF),
            pltpu.VMEM((C_TWO * C_PITCH, HX), F32),
            pltpu.VMEM((C_TWO * C_PITCH, HX), F32),
            pltpu.VMEM((144, C_ONE), F32),
            pltpu.VMEM((C_ONE, 4 * CELLS), F32),
            pltpu.VMEM((512, HX), F32),
        ],
        compiler_params=pltpu.CompilerParams(vmem_limit_bytes=48 * 1024 * 1024),
        interpret=interpret,
        name="slab",
    )(depth, *volumes, w1, b1, w2, b2, cot)


def split(total, interpret=False):
    return pl.pallas_call(
        unpack,
        out_shape=(
            jax.ShapeDtypeStruct((27, C_ONE, C_TWO), F32),
            jax.ShapeDtypeStruct((27, C_IN, C_ONE), F32),
            jax.ShapeDtypeStruct((1, C_ONE), F32),
            jax.ShapeDtypeStruct((1, C_TWO), F32),
        ),
        in_specs=[VMEM],
        out_specs=(VMEM,) * 4,
        interpret=interpret,
        name="unpack",
    )(total)


def per_device(volume, kernel_one, bias_one, kernel_two, bias_two, cotangent):
    volumes = (swapped(volume, 0), volume, swapped(volume, 1))
    depth = jnp.stack([lax.axis_index(DEPTH), lax.axis_size(DEPTH)]).astype(jnp.int32)
    w1 = jnp.transpose(kernel_one, (2, 3, 4, 1, 0)).reshape(27, C_IN, C_ONE)
    w2 = jnp.transpose(kernel_two, (2, 3, 4, 1, 0)).reshape(27, C_ONE, C_TWO)
    features, packed = local(depth, volumes, w1, bias_one[None], w2, bias_two[None], cotangent)
    two, one, b1, b2 = split(reduced(packed))
    two = jnp.transpose(two.reshape(3, 3, 3, C_ONE, C_TWO), (4, 3, 0, 1, 2))
    one = jnp.transpose(one.reshape(3, 3, 3, C_IN, C_ONE), (4, 3, 0, 1, 2))
    return (features, one, b1[0], two, b2[0])


def solution(mesh):
    cut = Mesh(mesh.devices.reshape(8, 2, 2, 4, 2), DP + DEPTH)
    return jax.shard_map(
        per_device,
        mesh=cut,
        in_specs=(
            P(DP, None, DEPTH, None, None),
            P(),
            P(),
            P(),
            P(),
            P(DP, None, DEPTH, None, None),
        ),
        out_specs=(P(DP, None, DEPTH, None, None), P(), P(), P(), P()),
        check_vma=False,
    )
```

time: 74.3 us -> 63.9 us (0.86)
  starting transfers between devices: 16.5 us -> 2.77 us
  blocking collectives: 45 us -> 48.5 us
  waiting for transfers between devices: 3.17 us -> 0.6 us
  local copies, waits for them, and re-layouts: 1.72 us -> 3.33 us
  Pallas kernels: 6.61 us -> 7.55 us
    ppermute x6 -> x2, starting transfers between devices: 16.5 us -> 2.77 us  [swapped(): return lax.ppermute(x, DEPTH, ups + [(j, i) for i, j in ups])]
    all_to_all x3, blocking collectives: 45 us -> 48.5 us  [exchange(): return lax.all_to_all(x, axes, 0, 0, tiled=True)]
    unnamed x12, local copies, waits for them, and re-layouts: 0.65 us -> 3.3 us
    ppermute x6 -> x2, waiting for transfers between devices: 3.17 us -> 0.6 us  [swapped(): return lax.ppermute(x, DEPTH, ups + [(j, i) for i, j in ups])]
    slice x1 -> x0, local copies, waits for them, and re-layouts: 1.04 us -> none  [per_device(): cotangent[:, :, :1]]
    pallas_call x1, Pallas kernels: 4.82 us -> 5.76 us  [local(): pl.pallas_call(compute, out_shape=(jax.ShapeDtypeStruct((1, C_TWO, 2, HY,...]
  transfers between devices with their start and end apart: 6 -> 2, of which waited for: 1 -> 1; matrix products, arithmetic and copies ran while one was open for 0% -> 0% of each run, Pallas kernels for 0% -> 0%
where the time goes in v3:
time: 63.9 us; the launch traced here: 63.5 us
  blocking collectives  48.5 us (76%)
  Pallas kernels  7.55 us (12%)
  local copies, waits for them, and re-layouts  3.33 us (5%)
  starting transfers between devices  2.77 us (4%)
  between operations  0.69 us (1%)
    all_to_all x3, blocking collectives, exchange(): return lax.all_to_all(x, axes, 0, 0, tiled=True)  48.5 us
    pallas_call x1, Pallas kernels, local(): pl.pallas_call(compute, out_shape=(jax.ShapeDtypeStruct((1, C_TWO, 2, HY,...  5.76 us
    unnamed x12, local copies, waits for them, and re-layouts  3.3 us
    ppermute x2, starting transfers between devices, swapped(): return lax.ppermute(x, DEPTH, ups + [(j, i) for i, j in ups])  2.77 us
    pallas_call x1, Pallas kernels, split(): pl.pallas_call(unpack, out_shape=(jax.ShapeDtypeStruct((27, C_ONE, C_TWO)...  1.79 us
  transfers between devices with their start and end apart: 2, of which 1 were waited for; matrix products, arithmetic and copies ran while one was open for 0% of the time, Pallas kernels for 0%

profile of v3, /device:TPU:1, one launch (start us, length us, event | category | flops | bytes accessed | tf_op | source)
XLA Modules:
  0.0 63.5 jit_solution(4539747268543390631)
XLA Ops:
  0.6 0.0 copy-start.3
  0.6 2.1 %collective-permute-start = (bf16[1,4,2,8,128]{4,3,2,1,0:T(8,128)(2,1)}, bf16[1,4,2,8,128]{4,3,2,1,0:T(8,128)(2,1)S(1)}, u32[]{:S(2)}, u32[]{:S(2)}) collective-permute-start(bf16[1,4,2,8,128]{4,3,2,1,0:T(8,128)(2,1)} %v0.1), channel_id=1, source_target_pairs={{0,1},{2,3},{4,5},{6,7},{1,0},{3,2},{5,4},{7,6},{8,9},{10,11},{12,... | collective-permute-start | bytes 49160 | tf_op jit(solution)/shard_map/ppermute | solution.py:202
  2.8 0.7 %collective-permute-start.1 = (bf16[1,4,2,8,128]{4,3,2,1,0:T(8,128)(2,1)}, bf16[1,4,2,8,128]{4,3,2,1,0:T(8,128)(2,1)S(1)}, u32[]{:S(2)}, u32[]{:S(2)}) collective-permute-start(bf16[1,4,2,8,128]{4,3,2,1,0:T(8,128)(2,1)} %v0.1), channel_id=1, source_target_pairs={{1,2},{3,4},{5,6},{2,1},{4,3},{6,5},{9,10},{11,12},{13,14},{10,9},... | collective-permute-start | bytes 49160 | tf_op jit(solution)/shard_map/ppermute | solution.py:202
  3.4 0.1 pad_add_fusion.depth
  3.5 0.6 collective-permute-done.va
  4.1 0.0 collective-permute-done.1.vb
  4.1 0.0 copy-start.4
  4.1 0.0 copy-start.5
  4.1 0.0 copy-done.3
  4.1 0.6 %copy-done.4 = f32[32]{0:T(128)S(1)} copy-done((f32[32]{0:T(128)S(1)}, f32[32]{0:T(128)}, u32[]{:S(2)}) %copy-start.4) | copy-done | bytes 152
  4.8 0.0 copy-done.5
  4.8 0.0 copy-start
  4.8 0.9 %copy-done = bf16[1,64,2,8,128]{4,3,2,1,0:T(8,128)(2,1)S(1)} copy-done((bf16[1,64,2,8,128]{4,3,2,1,0:T(8,128)(2,1)S(1)}, bf16[1,64,2,8,128]{4,3,2,1,0:T(8,128)(2,1)}, u32[]{:S(2)}) %copy-start) | copy-done | bytes 262168
  5.7 0.0 copy-start.1
  5.7 0.9 %copy-done.1 = bf16[64,32,3,3,3]{0,1,4,3,2:T(8,128)(2,1)S(1)} copy-done((bf16[64,32,3,3,3]{0,1,4,3,2:T(8,128)(2,1)S(1)}, bf16[64,32,3,3,3]{0,1,4,3,2:T(8,128)(2,1)}, u32[]{:S(2)}) %copy-start.1) | copy-done | bytes 110616
  6.7 0.0 copy-start.2
  6.7 0.7 %copy-done.2 = bf16[32,4,3,3,3]{0,1,4,3,2:T(4,128)(2,1)S(1)} copy-done((bf16[32,4,3,3,3]{0,1,4,3,2:T(4,128)(2,1)S(1)}, bf16[32,4,3,3,3]{0,1,4,3,2:T(4,128)(2,1)}, u32[]{:S(2)}) %copy-start.2) | copy-done | bytes 6936
  7.4 5.8 %slab.1 = (bf16[1,64,2,8,128]{4,3,2,1,0:T(8,128)(2,1)}, bf16[32,16,128]{2,1,0:T(8,128)(2,1)S(1)}) custom-call(s32[2]{0:T(128)S(1)} %pad_add_fusion.depth, bf16[1,4,2,8,128]{4,3,2,1,0:T(8,128)(2,1)S(1)} %collective-permute-done.va, bf16[1,4,2,8,128]{4,3,2,1,0:T(8,128)(2,1)S(1)} %copy-done.3, bf16[1,4,2,8,128]{4,3,2,1,0:T(8,128)(2,1)S(1)} %collective-permute-done.1.vb, ...), custom_call_target="tpu_custom_call" | custom-call | tf_op jit(solution)/shard_map/slab/pallas_call | solution.py:210
  13.2 20.7 %all_to_all.15 = bf16[32,16,128]{2,1,0:T(8,128)(2,1)S(1)} all-to-all(bf16[32,16,128]{2,1,0:T(8,128)(2,1)S(1)} %get-tuple-element.12), channel_id=1, replica_groups=mesh['z'=8,'x_hi'=2,'core'=2,'y'=4,'x_lo'=2] {'x_hi','core','y','x_lo'}, dimensions={0} | all-to-all | bytes 262144 | tf_op jit(solution)/shard_map/all_to_all | solution.py:186
  33.9 14.9 %all_to_all.16 = bf16[8,16,128]{2,1,0:T(8,128)(2,1)S(1)} all-to-all(bf16[8,16,128]{2,1,0:T(8,128)(2,1)S(1)} %broadcast_in_dim.20), channel_id=1, replica_groups=mesh['z'=8,'x_hi'=2,'core'=2,'y'=4,'x_lo'=2] {'z'}, dimensions={0} | all-to-all | bytes 65536 | tf_op jit(solution)/shard_map/all_to_all | solution.py:186
  48.9 12.9 %all_to_all.17.total = bf16[32,16,128]{2,1,0:T(8,128)(2,1)} all-to-all(bf16[32,16,128]{2,1,0:T(8,128)(2,1)S(1)} %broadcast_in_dim.21), channel_id=1, replica_groups=mesh['z'=8,'x_hi'=2,'core'=2,'y'=4,'x_lo'=2] {'x_hi','core','y','x_lo'}, dimensions={0} | all-to-all | bytes 262144 | tf_op jit(solution)/shard_map/all_to_all | solution.py:186
  61.8 1.8 %unpack.1 = (f32[27,32,64]{2,1,0:T(8,128)}, f32[27,4,32]{2,1,0:T(4,128)}, f32[1,32]{1,0:T(1,128)}, f32[1,64]{1,0:T(1,128)}) custom-call(bf16[32,16,128]{2,1,0:T(8,128)(2,1)} %all_to_all.17.total), custom_call_target="tpu_custom_call" | custom-call | tf_op jit(solution)/shard_map/unpack/pallas_call | solution.py:237
  (4 shorter events, 0.1 us)
Async XLA Ops:
  0.6 3.5 %copy-start.3 = (bf16[1,4,2,8,128]{4,3,2,1,0:T(8,128)(2,1)S(1)}, bf16[1,4,2,8,128]{4,3,2,1,0:T(8,128)(2,1)}, u32[]{:S(2)}) copy-start(bf16[1,4,2,8,128]{4,3,2,1,0:T(8,128)(2,1)} %v0.1) | copy-start | bytes 49156
  0.6 3.5 %collective-permute-start = (bf16[1,4,2,8,128]{4,3,2,1,0:T(8,128)(2,1)}, bf16[1,4,2,8,128]{4,3,2,1,0:T(8,128)(2,1)S(1)}, u32[]{:S(2)}, u32[]{:S(2)}) collective-permute-start(bf16[1,4,2,8,128]{4,3,2,1,0:T(8,128)(2,1)} %v0.1), channel_id=1, source_target_pairs={{0,1},{2,3},{4,5},{6,7},{1,0},{3,2},{5,4},{7,6},{8,9},{10,11},{12,... | collective-permute-start | bytes 49160 | tf_op jit(solution)/shard_map/ppermute | solution.py:202
  2.8 1.3 %collective-permute-start.1 = (bf16[1,4,2,8,128]{4,3,2,1,0:T(8,128)(2,1)}, bf16[1,4,2,8,128]{4,3,2,1,0:T(8,128)(2,1)S(1)}, u32[]{:S(2)}, u32[]{:S(2)}) collective-permute-start(bf16[1,4,2,8,128]{4,3,2,1,0:T(8,128)(2,1)} %v0.1), channel_id=1, source_target_pairs={{1,2},{3,4},{5,6},{2,1},{4,3},{6,5},{9,10},{11,12},{13,14},{10,9},... | collective-permute-start | bytes 49160 | tf_op jit(solution)/shard_map/ppermute | solution.py:202
  4.1 0.7 %copy-start.4 = (f32[32]{0:T(128)S(1)}, f32[32]{0:T(128)}, u32[]{:S(2)}) copy-start(f32[32]{0:T(128)} %param.8) | copy-start | bytes 388
  4.1 0.7 %copy-start.5 = (f32[64]{0:T(128)S(1)}, f32[64]{0:T(128)}, u32[]{:S(2)}) copy-start(f32[64]{0:T(128)} %param.10) | copy-start | bytes 772
  4.8 0.9 %copy-start = (bf16[1,64,2,8,128]{4,3,2,1,0:T(8,128)(2,1)S(1)}, bf16[1,64,2,8,128]{4,3,2,1,0:T(8,128)(2,1)}, u32[]{:S(2)}) copy-start(bf16[1,64,2,8,128]{4,3,2,1,0:T(8,128)(2,1)} %c0.1) | copy-start | bytes 786436
  5.7 0.9 %copy-start.1 = (bf16[64,32,3,3,3]{0,1,4,3,2:T(8,128)(2,1)S(1)}, bf16[64,32,3,3,3]{0,1,4,3,2:T(8,128)(2,1)}, u32[]{:S(2)}) copy-start(bf16[64,32,3,3,3]{0,1,4,3,2:T(8,128)(2,1)} %param.9) | copy-start | bytes 331780
  6.7 0.7 %copy-start.2 = (bf16[32,4,3,3,3]{0,1,4,3,2:T(4,128)(2,1)S(1)}, bf16[32,4,3,3,3]{0,1,4,3,2:T(4,128)(2,1)}, u32[]{:S(2)}) copy-start(bf16[32,4,3,3,3]{0,1,4,3,2:T(4,128)(2,1)} %param.7) | copy-start | bytes 20740

commit v4 on v3

--- a/solution.py
+++ b/solution.py
@@ -56,10 +56,39 @@
     return before, x, after
 
 
+def prepare(w1, b1, w2, b2, c0, w1t, w2t, flip, bias, cot, w1v, w2v, cv, bv1, bv2, w1s, cs, sems):
+    copies = [
+        pltpu.make_async_copy(src, dst, sems.at[n])
+        for n, (src, dst) in enumerate(((w1, w1v), (w2, w2v), (b1, bv1), (b2, bv2), (c0, cv)))
+    ]
+    for copy in copies:
+        copy.start()
+    w1s[...] = jnp.zeros((144, C_ONE), F32)
+    copies[0].wait()
+    for a in range(3):
+        for t in range(9):
+            w1s[a * 48 + t * 4 : a * 48 + t * 4 + 4, :] = w1v[a * 9 + t].astype(F32)
+        w1t[a * C_ONE : (a + 1) * C_ONE, :] = transposed(w1s[a * 48 : (a + 1) * 48, :].astype(BF))
+    copies[1].wait()
+    for k in range(9):
+        w2t[k * C_TWO : (k + 1) * C_TWO, :] = transposed(w2v[3 * k : 3 * k + 3].reshape(96, C_TWO))
+        flip[k * C_ONE : (k + 1) * C_ONE, :] = jnp.concatenate([w2v[(8 - k) * 3 + 2 - c] for c in range(3)], axis=1)
+    copies[2].wait()
+    copies[3].wait()
+    bias[0:C_ONE, :] = jnp.broadcast_to(column(bv1[...]), (C_ONE, HX))
+    bias[C_ONE:, :] = jnp.broadcast_to(column(bv2[...]), (C_TWO, HX))
+    copies[4].wait()
+    for o in range(C_TWO):
+        for z in range(2):
+            cs[o * C_PITCH + z * HY : o * C_PITCH + (z + 1) * HY, :] = cv[0, o, z].astype(F32)
+    for row in range(2 * HY):
+        cot[:, row * HX : (row + 1) * HX] = cs[pl.ds(row, C_TWO, stride=C_PITCH), :].astype(BF)
+
+
 def compute(
-    depth, va, v0, vb, w1, b1, w2, b2, c0,
+    depth, va, v0, vb, w1t, w2t, flip, bias, cot,
     features, packed,
-    vs, x1, x1b, x3, s3, cs, fs, w1s, p1, pk,
+    vs, x1, x1b, x3, s3, sb, fs, fb, p1, rs, pk, sem,
 ):
     even = depth[0] % 2 == 0
     for p in range(6):
@@ -84,19 +113,12 @@
                         col = p * CELLS + to * HX
                         x1[b * 12 + c * 4 : b * 12 + c * 4 + 4, col : col + HX] = moved
         x1b[:, p * CELLS : (p + 1) * CELLS] = x1[:, p * CELLS : (p + 1) * CELLS].astype(BF)
-    w1s[...] = jnp.zeros((144, C_ONE), F32)
-    for a in range(3):
-        for t in range(9):
-            w1s[a * 48 + t * 4 : a * 48 + t * 4 + 4, :] = w1[a * 9 + t].astype(F32)
-    w1t = [transposed(w1s[a * 48 : (a + 1) * 48, :].astype(BF)) for a in range(3)]
-    bias1 = column(b1[...])
-    bias2 = column(b2[...])
     for p in range(5):
         x3[:, p * ROWS * HX : p * ROWS * HX + HX] = jnp.zeros((96, HX), BF)
-    for q in range(3):
-        s3[:, q * ROWS * HX : q * ROWS * HX + HX] = jnp.zeros((192, HX), BF)
     for p in range(4):
-        pre = bias1 + sum(dot_nn(w1t[a], x1b[:, (p + a) * CELLS : (p + a + 1) * CELLS]) for a in range(3))
+        pre = bias[0:C_ONE, 0:1]
+        for a in range(3):
+            pre = pre + dot_nn(w1t[a * C_ONE : (a + 1) * C_ONE, :], x1b[:, (p + a) * CELLS : (p + a + 1) * CELLS])
         sig = sigmoid(pre)
         slope = sig * (1.0 + pre * (1.0 - sig))
         act = pre * sig
@@ -109,64 +131,74 @@
             col = (1 + p * ROWS + y) * HX
             for c, moved in enumerate(neighbours(act[:, y * HX : (y + 1) * HX])):
                 x3[c * C_ONE : (c + 1) * C_ONE, col : col + HX] = moved.astype(BF)
-    for z in range(2):
-        for o in range(C_TWO):
-            cs[o * C_PITCH + z * HY : o * C_PITCH + (z + 1) * HY, :] = c0[0, o, z].astype(F32)
-    w2t = [transposed(w2[3 * k : 3 * k + 3].reshape(96, C_TWO)) for k in range(9)]
     for q in range(2):
-        pre = bias2
+        sb[0:C_TWO, q * CELLS + 7 * HX : (q + 1) * CELLS] = jnp.zeros((C_TWO, HX), BF)
+        sb[2 * C_TWO :, q * CELLS : q * CELLS + HX] = jnp.zeros((C_TWO, HX), BF)
+        pre = bias[C_ONE:, 0:1]
         for k in range(9):
             col = ((q + k // 3) * ROWS + k % 3) * HX
-            pre = pre + dot_nn(w2t[k], x3[:, col : col + CELLS])
+            pre = pre + dot_nn(w2t[k * C_TWO : (k + 1) * C_TWO, :], x3[:, col : col + CELLS])
         sig = sigmoid(pre)
         slope = sig * (1.0 + pre * (1.0 - sig))
         act = pre * sig
         for y in range(HY):
             row = q * HY + y
-            cot = cs[pl.ds(row, C_TWO, stride=C_PITCH), :]
-            here = (cot * slope[:, y * HX : (y + 1) * HX]).astype(BF).astype(F32)
-            col = (1 + q * ROWS + y) * HX
-            for c, moved in enumerate(neighbours(here)):
+            col = row * HX
+            up = cot[:, col : col + HX].astype(F32)
+            here = (up * slope[:, y * HX : (y + 1) * HX]).astype(BF)
+            for b in range(3):
+                to = y + b - 1
+                if 0 <= to < HY:
+                    sb[b * C_TWO : (b + 1) * C_TWO, q * CELLS + to * HX : q * CELLS + (to + 1) * HX] = here
+            for c, moved in enumerate(neighbours(here.astype(F32))):
                 s3[c * C_TWO : (c + 1) * C_TWO, col : col + HX] = moved.astype(BF)
             fs[pl.ds(row, C_TWO, stride=C_PITCH), :] = act[:, y * HX : (y + 1) * HX]
     for o in range(C_TWO):
         for z in range(2):
-            features[0, o, z] = fs[o * C_PITCH + z * HY : o * C_PITCH + (z + 1) * HY, :].astype(BF)
-    mine = [s3[C_TWO : 2 * C_TWO, (1 + q * ROWS) * HX : (1 + q * ROWS) * HX + CELLS] for q in range(2)]
+            fb[0, o, z] = fs[o * C_PITCH + z * HY : o * C_PITCH + (z + 1) * HY, :].astype(BF)
+    out = pltpu.make_async_copy(fb, features, sem)
+    out.start()
+    for j in range(2):
+        rs[:, j * CELLS : (j + 1) * CELLS] = dot_nn(flip[...], s3[:, j * CELLS : (j + 1) * CELLS])
     pk[384:512, :] = jnp.zeros((128, HX), F32)
-    for k in range(9):
+    for a in range(3):
         grad = 0.0
         for j in range(2):
-            col = ((j + k // 3) * ROWS + k % 3) * HX
-            grad = grad + dot_nt(x3[:, col : col + CELLS], mine[j])
-        row, lane = place(k)
-        pk[row : row + 96, lane : lane + C_TWO] = grad
-    ones = jnp.ones((8, CELLS), BF)
-    pk[480:488, 0:C_TWO] = dot_nt(ones, mine[0]) + dot_nt(ones, mine[1])
-    flipped = []
-    for k in range(9):
-        flipped.append(jnp.concatenate([w2[(8 - k) * 3 + 2 - c] for c in range(3)], axis=1))
-    grads = [0.0, 0.0, 0.0]
+            col = (1 + (j + a) * ROWS) * HX
+            grad = grad + dot_nt(x3[:, col : col + CELLS], sb[:, j * CELLS : (j + 1) * CELLS])
+        for b in range(3):
+            row, lane = place(a * 3 + b)
+            pk[row : row + 96, lane : lane + C_TWO] = grad[:, b * C_TWO : (b + 1) * C_TWO]
+    ones = jnp.ones((8, 2 * CELLS), BF)
+    pk[480:488, 0:C_TWO] = dot_nt(ones, s3[C_TWO : 2 * C_TWO, :])
+    grads = 0.0
     for t in range(4):
-        back = 0.0
-        for k in range(9):
-            j = t + k // 3 - 2
-            if 0 <= j < 2:
-                col = (j * ROWS + k % 3) * HX
-                back = back + dot_nn(flipped[k], s3[:, col : col + CELLS])
-        share = back * p1[:, t * CELLS : (t + 1) * CELLS]
+        shares = []
+        for y in range(HY):
+            back = 0.0
+            for k in range(9):
+                j, row = t + k // 3 - 2, y + k % 3 - 1
+                if 0 <= j < 2 and 0 <= row < HY:
+                    col = j * CELLS + row * HX
+                    back = back + rs[k * C_ONE : (k + 1) * C_ONE, col : col + HX]
+            shares.append(back * p1[:, t * CELLS + y * HX : t * CELLS + (y + 1) * HX])
+        share = jnp.concatenate(shares, axis=1)
         high = share.astype(BF)
         share = jnp.concatenate([high, (share - high.astype(F32)).astype(BF)], axis=0)
-        for a in range(3):
-            grads[a] = grads[a] + dot_nt(x1b[:, (t + a) * CELLS : (t + a + 1) * CELLS], share)
+        near = jnp.concatenate([x1b[:, (t + a) * CELLS : (t + a + 1) * CELLS] for a in range(3)], axis=0)
+        grads = grads + dot_nt(near, share)
     for a in range(3):
-        grad = grads[a][:40]
+        grad = grads[a * 48 : a * 48 + 40]
         pk[384 + a * 40 : 384 + a * 40 + 40, C_TWO : C_TWO + C_ONE] = grad[:, :C_ONE] + grad[:, C_ONE:]
     packed[...] = pk[...].astype(BF).reshape(32, 16, HX)
+    out.wait()
 
 
 def place(k):
-    return ((k % 4) * 96, (k // 4) * C_TWO) if k < 8 else (384, 0)
+    a, b = k // 3, k % 3
+    if b < 2:
+        return a * 96, b * C_TWO
+    return (288, a * C_TWO) if a < 2 else (384, 0)
 
 
 def unpack(total, two, one, bias_one, bias_two):
@@ -203,10 +235,37 @@
 
 
 VMEM = pl.BlockSpec(memory_space=pltpu.VMEM)
+HBM = pl.BlockSpec(memory_space=pltpu.HBM)
 SMEM = pl.BlockSpec(memory_space=pltpu.SMEM)
 
 
 def local(depth, volumes, w1, b1, w2, b2, cot, interpret=False):
+    held = [x if interpret else pltpu.with_memory_space_constraint(x, pltpu.HBM) for x in (w1, b1, w2, b2, cot)]
+    ready = pl.pallas_call(
+        prepare,
+        out_shape=(
+            jax.ShapeDtypeStruct((96, 48), BF),
+            jax.ShapeDtypeStruct((576, 96), BF),
+            jax.ShapeDtypeStruct((288, 192), BF),
+            jax.ShapeDtypeStruct((96, HX), F32),
+            jax.ShapeDtypeStruct((C_TWO, 2 * CELLS), BF),
+        ),
+        in_specs=[HBM] * 5,
+        out_specs=(VMEM,) * 5,
+        scratch_shapes=[
+            pltpu.VMEM((27, C_IN, C_ONE), BF),
+            pltpu.VMEM((27, C_ONE, C_TWO), BF),
+            pltpu.VMEM((1, C_TWO, 2, HY, HX), BF),
+            pltpu.VMEM((1, C_ONE), F32),
+            pltpu.VMEM((1, C_TWO), F32),
+            pltpu.VMEM((144, C_ONE), F32),
+            pltpu.VMEM((C_TWO * C_PITCH, HX), F32),
+            pltpu.SemaphoreType.DMA((5,)),
+        ],
+        compiler_params=pltpu.CompilerParams(vmem_limit_bytes=16 * 1024 * 1024),
+        interpret=interpret,
+        name="prepare",
+    )(*held)
     return pl.pallas_call(
         compute,
         out_shape=(
@@ -214,23 +273,25 @@
             jax.ShapeDtypeStruct((32, 16, HX), BF),
         ),
         in_specs=[SMEM] + [VMEM] * 8,
-        out_specs=(VMEM, VMEM),
+        out_specs=(HBM, VMEM),
         scratch_shapes=[
             pltpu.VMEM((C_IN * V_PITCH, HX), F32),
             pltpu.VMEM((48, 6 * CELLS), F32),
             pltpu.VMEM((48, 6 * CELLS), BF),
             pltpu.VMEM((96, 37 * HX), BF),
-            pltpu.VMEM((192, 19 * HX), BF),
+            pltpu.VMEM((192, 2 * CELLS), BF),
+            pltpu.VMEM((192, 2 * CELLS), BF),
             pltpu.VMEM((C_TWO * C_PITCH, HX), F32),
-            pltpu.VMEM((C_TWO * C_PITCH, HX), F32),
-            pltpu.VMEM((144, C_ONE), F32),
+            pltpu.VMEM((1, C_TWO, 2, HY, HX), BF),
             pltpu.VMEM((C_ONE, 4 * CELLS), F32),
+            pltpu.VMEM((288, 2 * CELLS), F32),
             pltpu.VMEM((512, HX), F32),
+            pltpu.SemaphoreType.DMA,
         ],
-        compiler_params=pltpu.CompilerParams(vmem_limit_bytes=48 * 1024 * 1024),
+        compiler_params=pltpu.CompilerParams(vmem_limit_bytes=24 * 1024 * 1024),
         interpret=interpret,
         name="slab",
-    )(depth, *volumes, w1, b1, w2, b2, cot)
+    )(depth, *volumes, *ready)
 
 
 def split(total, interpret=False):
@@ -244,6 +305,7 @@
         ),
         in_specs=[VMEM],
         out_specs=(VMEM,) * 4,
+        compiler_params=pltpu.CompilerParams(vmem_limit_bytes=4 * 1024 * 1024),
         interpret=interpret,
         name="unpack",
     )(total)

time: 63.9 us -> 57.5 us (0.90)
  local copies, waits for them, and re-layouts: 3.33 us -> 0.03 us
  Pallas kernels: 7.55 us -> 6.23 us
  blocking collectives: 48.5 us -> 47.4 us
    unnamed x12 -> x2, local copies, waits for them, and re-layouts: 3.3 us -> 0.01 us
    pallas_call x1, Pallas kernels: 5.76 us -> 3.83 us  [local(): pl.pallas_call(compute, out_shape=(jax.ShapeDtypeStruct((1, C_TWO, 2, HY,...]
    pallas_call x0 -> x1, Pallas kernels: none -> 1.52 us  [local(): pl.pallas_call(prepare, out_shape=(jax.ShapeDtypeStruct((96, 48), BF), ja...]
    all_to_all x3, blocking collectives: 48.5 us -> 47.4 us  [exchange(): return lax.all_to_all(x, axes, 0, 0, tiled=True)]
    pallas_call x1, Pallas kernels: 1.79 us -> 0.88 us  [split(): pl.pallas_call(unpack, out_shape=(jax.ShapeDtypeStruct((27, C_ONE, C_TWO)...]
  transfers between devices with their start and end apart: 2 -> 2, of which waited for: 1 -> 0; matrix products, arithmetic and copies ran while one was open for 0% -> 0% of each run, Pallas kernels for 0% -> 3%
where the time goes in v4:
time: 57.5 us; the launch traced here: 57.3 us
  blocking collectives  47.4 us (82%)
  Pallas kernels  6.23 us (11%)
  starting transfers between devices  2.77 us (5%)
  between operations  0.71 us (1%)
    all_to_all x3, blocking collectives, exchange(): return lax.all_to_all(x, axes, 0, 0, tiled=True)  47.4 us
    pallas_call x1, Pallas kernels, local(): pl.pallas_call(compute, out_shape=(jax.ShapeDtypeStruct((1, C_TWO, 2, HY,...  3.83 us
    ppermute x2, starting transfers between devices, swapped(): return lax.ppermute(x, DEPTH, ups + [(j, i) for i, j in ups])  2.77 us
    pallas_call x1, Pallas kernels, local(): pl.pallas_call(prepare, out_shape=(jax.ShapeDtypeStruct((96, 48), BF), ja...  1.52 us
  transfers between devices with their start and end apart: 2, of which 0 were waited for; matrix products, arithmetic and copies ran while one was open for 0% of the time, Pallas kernels for 3%

profile of v4, /device:TPU:1, one launch (start us, length us, event | category | flops | bytes accessed | tf_op | source)
XLA Modules:
  0.0 57.3 jit_solution(6430833842244666323)
XLA Ops:
  0.6 2.1 %collective-permute-start = (bf16[1,4,2,8,128]{4,3,2,1,0:T(8,128)(2,1)}, bf16[1,4,2,8,128]{4,3,2,1,0:T(8,128)(2,1)S(1)}, u32[]{:S(2)}, u32[]{:S(2)}) collective-permute-start(bf16[1,4,2,8,128]{4,3,2,1,0:T(8,128)(2,1)} %v0.1), channel_id=1, source_target_pairs={{0,1},{2,3},{4,5},{6,7},{1,0},{3,2},{5,4},{7,6},{8,9},{10,11},{12,... | collective-permute-start | bytes 49160 | tf_op jit(solution)/shard_map/ppermute | solution.py:234
  2.7 0.7 %collective-permute-start.1 = (bf16[1,4,2,8,128]{4,3,2,1,0:T(8,128)(2,1)}, bf16[1,4,2,8,128]{4,3,2,1,0:T(8,128)(2,1)S(1)}, u32[]{:S(2)}, u32[]{:S(2)}) collective-permute-start(bf16[1,4,2,8,128]{4,3,2,1,0:T(8,128)(2,1)} %v0.1), channel_id=1, source_target_pairs={{1,2},{3,4},{5,6},{2,1},{4,3},{6,5},{9,10},{11,12},{13,14},{10,9},... | collective-permute-start | bytes 49160 | tf_op jit(solution)/shard_map/ppermute | solution.py:234
  3.4 0.1 pad_add_fusion.depth
  3.5 0.0 copy-start
  3.5 1.5 %prepare.1 = (bf16[96,48]{1,0:T(8,128)(2,1)S(1)}, bf16[576,96]{1,0:T(8,128)(2,1)S(1)}, bf16[288,192]{1,0:T(8,128)(2,1)S(1)}, f32[96,128]{1,0:T(8,128)S(1)}, bf16[64,2048]{1,0:T(8,128)(2,1)S(1)}) custom-call(bf16[27,4,32]{2,1,0:T(4,128)(2,1)} %bitcast.18, f32[1,32]{1,0:T(1,128)} %bitcast.19, bf16[27,32,64]{2,1,0:T(8,128)(2,1)} %bitcast.17, f32[1,64]{1,0:T(1,128)} %bitcast.20, ...), custom_call_target="tpu_custom_call" | custom-call | tf_op jit(solution)/shard_map/prepare/pallas_call | solution.py:244
  5.0 0.0 collective-permute-done.va
  5.0 0.0 collective-permute-done.1.vb
  5.0 0.0 copy-done
  5.0 3.8 %slab.1 = (bf16[1,64,2,8,128]{4,3,2,1,0:T(8,128)(2,1)}, bf16[32,16,128]{2,1,0:T(8,128)(2,1)S(1)}) custom-call(s32[2]{0:T(128)S(1)} %pad_add_fusion.depth, bf16[1,4,2,8,128]{4,3,2,1,0:T(8,128)(2,1)S(1)} %collective-permute-done.va, bf16[1,4,2,8,128]{4,3,2,1,0:T(8,128)(2,1)S(1)} %copy-done, bf16[1,4,2,8,128]{4,3,2,1,0:T(8,128)(2,1)S(1)} %collective-permute-done.1.vb, ...), custom_call_target="tpu_custom_call" | custom-call | tf_op jit(solution)/shard_map/slab/pallas_call | solution.py:269
  8.9 19.7 %all_to_all.15 = bf16[32,16,128]{2,1,0:T(8,128)(2,1)S(1)} all-to-all(bf16[32,16,128]{2,1,0:T(8,128)(2,1)S(1)} %get-tuple-element.22), channel_id=1, replica_groups=mesh['z'=8,'x_hi'=2,'core'=2,'y'=4,'x_lo'=2] {'x_hi','core','y','x_lo'}, dimensions={0} | all-to-all | bytes 262144 | tf_op jit(solution)/shard_map/all_to_all | solution.py:218
  28.6 15.0 %all_to_all.16 = bf16[8,16,128]{2,1,0:T(8,128)(2,1)S(1)} all-to-all(bf16[8,16,128]{2,1,0:T(8,128)(2,1)S(1)} %broadcast_in_dim.20), channel_id=1, replica_groups=mesh['z'=8,'x_hi'=2,'core'=2,'y'=4,'x_lo'=2] {'z'}, dimensions={0} | all-to-all | bytes 65536 | tf_op jit(solution)/shard_map/all_to_all | solution.py:218
  43.6 12.8 %all_to_all.17.total = bf16[32,16,128]{2,1,0:T(8,128)(2,1)S(1)} all-to-all(bf16[32,16,128]{2,1,0:T(8,128)(2,1)S(1)} %broadcast_in_dim.21), channel_id=1, replica_groups=mesh['z'=8,'x_hi'=2,'core'=2,'y'=4,'x_lo'=2] {'x_hi','core','y','x_lo'}, dimensions={0} | all-to-all | bytes 262144 | tf_op jit(solution)/shard_map/all_to_all | solution.py:218
  56.4 0.9 %unpack.1 = (f32[27,32,64]{2,1,0:T(8,128)}, f32[27,4,32]{2,1,0:T(4,128)}, f32[1,32]{1,0:T(1,128)}, f32[1,64]{1,0:T(1,128)}) custom-call(bf16[32,16,128]{2,1,0:T(8,128)(2,1)S(1)} %all_to_all.17.total), custom_call_target="tpu_custom_call" | custom-call | tf_op jit(solution)/shard_map/unpack/pallas_call | solution.py:298
  (4 shorter events, 0.1 us)
Async XLA Ops:
  0.6 4.4 %collective-permute-start = (bf16[1,4,2,8,128]{4,3,2,1,0:T(8,128)(2,1)}, bf16[1,4,2,8,128]{4,3,2,1,0:T(8,128)(2,1)S(1)}, u32[]{:S(2)}, u32[]{:S(2)}) collective-permute-start(bf16[1,4,2,8,128]{4,3,2,1,0:T(8,128)(2,1)} %v0.1), channel_id=1, source_target_pairs={{0,1},{2,3},{4,5},{6,7},{1,0},{3,2},{5,4},{7,6},{8,9},{10,11},{12,... | collective-permute-start | bytes 49160 | tf_op jit(solution)/shard_map/ppermute | solution.py:234
  2.7 2.3 %collective-permute-start.1 = (bf16[1,4,2,8,128]{4,3,2,1,0:T(8,128)(2,1)}, bf16[1,4,2,8,128]{4,3,2,1,0:T(8,128)(2,1)S(1)}, u32[]{:S(2)}, u32[]{:S(2)}) collective-permute-start(bf16[1,4,2,8,128]{4,3,2,1,0:T(8,128)(2,1)} %v0.1), channel_id=1, source_target_pairs={{1,2},{3,4},{5,6},{2,1},{4,3},{6,5},{9,10},{11,12},{13,14},{10,9},... | collective-permute-start | bytes 49160 | tf_op jit(solution)/shard_map/ppermute | solution.py:234
  3.5 1.6 %copy-start = (bf16[1,4,2,8,128]{4,3,2,1,0:T(8,128)(2,1)S(1)}, bf16[1,4,2,8,128]{4,3,2,1,0:T(8,128)(2,1)}, u32[]{:S(2)}) copy-start(bf16[1,4,2,8,128]{4,3,2,1,0:T(8,128)(2,1)} %v0.1) | copy-start | bytes 49156

commit v5 on v4

--- a/solution.py
+++ b/solution.py
@@ -9,7 +9,7 @@
 DP = ("z", "x_hi", "core")
 DEPTH = ("y", "x_lo")
 PLANE = ("x_hi", "core", "y", "x_lo")
-LINE = "z"
+LINE = ("z",)
 
 BF = jnp.bfloat16
 F32 = jnp.float32
@@ -214,18 +214,27 @@
     bias_two[...] = flat[480:481, 0:64]
 
 
-def exchange(x, axes):
-    return lax.all_to_all(x, axes, 0, 0, tiled=True)
+def exchange(x, axes, first):
+    order = [first] + [i for i in range(lax.axis_size(axes)) if i != first]
+    return lax.all_to_all(x, axes, 0, 0, axis_index_groups=[order], tiled=True)
+
+
+def middle(axes):
+    index = 0
+    for axis in axes:
+        size = lax.axis_size(axis)
+        index = index * size + {"x_hi": 1, "x_lo": 0, "core": 1}.get(axis, size // 2)
+    return index
 
 
 def reduced(x):
     plane = lax.axis_size(PLANE)
     line = lax.axis_size(LINE)
-    part = exchange(x, PLANE)
+    part = exchange(x, PLANE, middle(PLANE))
     part = jnp.sum(part, axis=0, dtype=F32).astype(x.dtype)
-    part = exchange(jnp.broadcast_to(part[None], (line,) + part.shape), LINE)
+    part = exchange(jnp.broadcast_to(part[None], (line,) + part.shape), LINE, middle(LINE))
     part = jnp.sum(part, axis=0, dtype=F32).astype(x.dtype)
-    return exchange(jnp.broadcast_to(part[None], (plane,) + part.shape), PLANE)
+    return exchange(jnp.broadcast_to(part[None], (plane,) + part.shape), PLANE, middle(PLANE))
 
 
 def swapped(x, first):

time: 57.5 us -> 49.5 us (0.86)
  blocking collectives: 47.4 us -> 39.4 us
    all_to_all x3, blocking collectives: 47.4 us -> 39.4 us  [exchange(): return lax.all_to_all(x, axes, 0, 0, axis_index_groups=[order], tiled=True)]
where the time goes in v5:
time: 49.5 us; the launch traced here: 49.3 us
  blocking collectives  39.4 us (80%)
  Pallas kernels  6.23 us (13%)
  starting transfers between devices  2.77 us (6%)
  between operations  0.71 us (1%)
    all_to_all x3, blocking collectives, exchange(): return lax.all_to_all(x, axes, 0, 0, axis_index_groups=[order], tiled=True)  39.4 us
    pallas_call x1, Pallas kernels, local(): pl.pallas_call(compute, out_shape=(jax.ShapeDtypeStruct((1, C_TWO, 2, HY,...  3.83 us
    ppermute x2, starting transfers between devices, swapped(): return lax.ppermute(x, DEPTH, ups + [(j, i) for i, j in ups])  2.77 us
    pallas_call x1, Pallas kernels, local(): pl.pallas_call(prepare, out_shape=(jax.ShapeDtypeStruct((96, 48), BF), ja...  1.52 us
  transfers between devices with their start and end apart: 2, of which 0 were waited for; matrix products, arithmetic and copies ran while one was open for 0% of the time, Pallas kernels for 3%

profile of v5, /device:TPU:1, one launch (start us, length us, event | category | flops | bytes accessed | tf_op | source)
XLA Modules:
  0.0 49.3 jit_solution(11491117677071314997)
XLA Ops:
  0.6 2.1 %collective-permute-start = (bf16[1,4,2,8,128]{4,3,2,1,0:T(8,128)(2,1)}, bf16[1,4,2,8,128]{4,3,2,1,0:T(8,128)(2,1)S(1)}, u32[]{:S(2)}, u32[]{:S(2)}) collective-permute-start(bf16[1,4,2,8,128]{4,3,2,1,0:T(8,128)(2,1)} %v0.1), channel_id=1, source_target_pairs={{0,1},{2,3},{4,5},{6,7},{1,0},{3,2},{5,4},{7,6},{8,9},{10,11},{12,... | collective-permute-start | bytes 49160 | tf_op jit(solution)/shard_map/ppermute | solution.py:243
  2.7 0.7 %collective-permute-start.1 = (bf16[1,4,2,8,128]{4,3,2,1,0:T(8,128)(2,1)}, bf16[1,4,2,8,128]{4,3,2,1,0:T(8,128)(2,1)S(1)}, u32[]{:S(2)}, u32[]{:S(2)}) collective-permute-start(bf16[1,4,2,8,128]{4,3,2,1,0:T(8,128)(2,1)} %v0.1), channel_id=1, source_target_pairs={{1,2},{3,4},{5,6},{2,1},{4,3},{6,5},{9,10},{11,12},{13,14},{10,9},... | collective-permute-start | bytes 49160 | tf_op jit(solution)/shard_map/ppermute | solution.py:243
  3.4 0.1 pad_add_fusion.depth
  3.5 0.0 copy-start
  3.5 1.5 %prepare.1 = (bf16[96,48]{1,0:T(8,128)(2,1)S(1)}, bf16[576,96]{1,0:T(8,128)(2,1)S(1)}, bf16[288,192]{1,0:T(8,128)(2,1)S(1)}, f32[96,128]{1,0:T(8,128)S(1)}, bf16[64,2048]{1,0:T(8,128)(2,1)S(1)}) custom-call(bf16[27,4,32]{2,1,0:T(4,128)(2,1)} %bitcast.18, f32[1,32]{1,0:T(1,128)} %bitcast.19, bf16[27,32,64]{2,1,0:T(8,128)(2,1)} %bitcast.17, f32[1,64]{1,0:T(1,128)} %bitcast.20, ...), custom_call_target="tpu_custom_call" | custom-call | tf_op jit(solution)/shard_map/prepare/pallas_call | solution.py:253
  5.0 0.0 collective-permute-done.va
  5.0 0.0 collective-permute-done.1.vb
  5.0 0.0 copy-done
  5.0 3.8 %slab.1 = (bf16[1,64,2,8,128]{4,3,2,1,0:T(8,128)(2,1)}, bf16[32,16,128]{2,1,0:T(8,128)(2,1)S(1)}) custom-call(s32[2]{0:T(128)S(1)} %pad_add_fusion.depth, bf16[1,4,2,8,128]{4,3,2,1,0:T(8,128)(2,1)S(1)} %collective-permute-done.va, bf16[1,4,2,8,128]{4,3,2,1,0:T(8,128)(2,1)S(1)} %copy-done, bf16[1,4,2,8,128]{4,3,2,1,0:T(8,128)(2,1)S(1)} %collective-permute-done.1.vb, ...), custom_call_target="tpu_custom_call" | custom-call | tf_op jit(solution)/shard_map/slab/pallas_call | solution.py:278
  8.9 15.8 %all_to_all.15 = bf16[32,16,128]{2,1,0:T(8,128)(2,1)S(1)} all-to-all(bf16[32,16,128]{2,1,0:T(8,128)(2,1)S(1)} %get-tuple-element.22), channel_id=1, replica_groups={{28,0,1,2,3,4,5,6,7,8,9,10,11,12,13,14,15,16,17,18,19,20,21,22,23,24,25..., dimensions={0} | all-to-all | bytes 262144 | tf_op jit(solution)/shard_map/all_to_all | solution.py:219
  24.8 11.5 %all_to_all.16 = bf16[8,16,128]{2,1,0:T(8,128)(2,1)S(1)} all-to-all(bf16[8,16,128]{2,1,0:T(8,128)(2,1)S(1)} %broadcast_in_dim.20), channel_id=1, replica_groups={{128,0,32,64,96,160,192,224},{129,1,33,65,97,161,193,225},{130,2,34,66,..., dimensions={0} | all-to-all | bytes 65536 | tf_op jit(solution)/shard_map/all_to_all | solution.py:219
  36.3 12.1 %all_to_all.17.total = bf16[32,16,128]{2,1,0:T(8,128)(2,1)S(1)} all-to-all(bf16[32,16,128]{2,1,0:T(8,128)(2,1)S(1)} %broadcast_in_dim.21), channel_id=1, replica_groups={{28,0,1,2,3,4,5,6,7,8,9,10,11,12,13,14,15,16,17,18,19,20,21,22,23,24,25..., dimensions={0} | all-to-all | bytes 262144 | tf_op jit(solution)/shard_map/all_to_all | solution.py:219
  48.4 0.9 %unpack.1 = (f32[27,32,64]{2,1,0:T(8,128)}, f32[27,4,32]{2,1,0:T(4,128)}, f32[1,32]{1,0:T(1,128)}, f32[1,64]{1,0:T(1,128)}) custom-call(bf16[32,16,128]{2,1,0:T(8,128)(2,1)S(1)} %all_to_all.17.total), custom_call_target="tpu_custom_call" | custom-call | tf_op jit(solution)/shard_map/unpack/pallas_call | solution.py:307
  (4 shorter events, 0.1 us)
Async XLA Ops:
  0.6 4.4 %collective-permute-start = (bf16[1,4,2,8,128]{4,3,2,1,0:T(8,128)(2,1)}, bf16[1,4,2,8,128]{4,3,2,1,0:T(8,128)(2,1)S(1)}, u32[]{:S(2)}, u32[]{:S(2)}) collective-permute-start(bf16[1,4,2,8,128]{4,3,2,1,0:T(8,128)(2,1)} %v0.1), channel_id=1, source_target_pairs={{0,1},{2,3},{4,5},{6,7},{1,0},{3,2},{5,4},{7,6},{8,9},{10,11},{12,... | collective-permute-start | bytes 49160 | tf_op jit(solution)/shard_map/ppermute | solution.py:243
  2.7 2.3 %collective-permute-start.1 = (bf16[1,4,2,8,128]{4,3,2,1,0:T(8,128)(2,1)}, bf16[1,4,2,8,128]{4,3,2,1,0:T(8,128)(2,1)S(1)}, u32[]{:S(2)}, u32[]{:S(2)}) collective-permute-start(bf16[1,4,2,8,128]{4,3,2,1,0:T(8,128)(2,1)} %v0.1), channel_id=1, source_target_pairs={{1,2},{3,4},{5,6},{2,1},{4,3},{6,5},{9,10},{11,12},{13,14},{10,9},... | collective-permute-start | bytes 49160 | tf_op jit(solution)/shard_map/ppermute | solution.py:243
  3.5 1.6 %copy-start = (bf16[1,4,2,8,128]{4,3,2,1,0:T(8,128)(2,1)S(1)}, bf16[1,4,2,8,128]{4,3,2,1,0:T(8,128)(2,1)}, u32[]{:S(2)}) copy-start(bf16[1,4,2,8,128]{4,3,2,1,0:T(8,128)(2,1)} %v0.1) | copy-start | bytes 49156

commit v6 on v5

--- a/solution.py
+++ b/solution.py
@@ -20,6 +20,7 @@
 C_IN = 4
 C_ONE = 32
 C_TWO = 64
+STEP = 8
 V_PITCH = 56
 C_PITCH = 24
 
@@ -67,11 +68,12 @@
     copies[0].wait()
     for a in range(3):
         for t in range(9):
-            w1s[a * 48 + t * 4 : a * 48 + t * 4 + 4, :] = w1v[a * 9 + t].astype(F32)
-        w1t[a * C_ONE : (a + 1) * C_ONE, :] = transposed(w1s[a * 48 : (a + 1) * 48, :].astype(BF))
+            row = a * 48 + t // 3 * 16 + t % 3 * 4
+            w1s[row : row + 4, :] = w1v[a * 9 + t].astype(F32)
+    w1t[...] = transposed(w1s[...].astype(BF))
     copies[1].wait()
+    w2t[...] = transposed(w2v[...].reshape(864, C_TWO))
     for k in range(9):
-        w2t[k * C_TWO : (k + 1) * C_TWO, :] = transposed(w2v[3 * k : 3 * k + 3].reshape(96, C_TWO))
         flip[k * C_ONE : (k + 1) * C_ONE, :] = jnp.concatenate([w2v[(8 - k) * 3 + 2 - c] for c in range(3)], axis=1)
     copies[2].wait()
     copies[3].wait()
@@ -88,7 +90,7 @@
 def compute(
     depth, va, v0, vb, w1t, w2t, flip, bias, cot,
     features, packed,
-    vs, x1, x1b, x3, s3, sb, fs, fb, p1, rs, pk, sem,
+    vs, x1b, x3, s3, sb, fs, fb, p1, rs, pk, sem,
 ):
     even = depth[0] % 2 == 0
     for p in range(6):
@@ -100,25 +102,27 @@
                 far = vb[0, i, p % 2].astype(F32)
                 plane = jnp.where(even, far, near) if p < 2 else jnp.where(even, near, far)
             vs[i * V_PITCH + p * HY : i * V_PITCH + (p + 1) * HY, :] = plane
-    x1[36:48, :] = jnp.where(lax.broadcasted_iota(jnp.int32, (12, 6 * CELLS), 0) == 0, 1.0, 0.0)
+    last = jnp.where(lax.broadcasted_iota(jnp.int32, (4, HX), 0) == 0, 1.0, 0.0)
+    edge = jnp.concatenate([jnp.zeros((12, HX), F32), last], axis=0).astype(BF)
     for p in range(6):
-        x1[0:12, p * CELLS : p * CELLS + HX] = jnp.zeros((12, HX), F32)
-        x1[24:36, p * CELLS + 7 * HX : (p + 1) * CELLS] = jnp.zeros((12, HX), F32)
+        x1b[0:16, p * CELLS : p * CELLS + HX] = edge
+        x1b[32:48, p * CELLS + 7 * HX : (p + 1) * CELLS] = edge
         for y in range(HY):
-            slab = vs[pl.ds(p * HY + y, C_IN, stride=V_PITCH), :]
-            for c, moved in enumerate(neighbours(slab)):
-                for b in range(3):
-                    to = y + 1 - b
-                    if 0 <= to < HY:
-                        col = p * CELLS + to * HX
-                        x1[b * 12 + c * 4 : b * 12 + c * 4 + 4, col : col + HX] = moved
-        x1b[:, p * CELLS : (p + 1) * CELLS] = x1[:, p * CELLS : (p + 1) * CELLS].astype(BF)
+            before, slab, after = neighbours(vs[pl.ds(p * HY + y, C_IN, stride=V_PITCH), :])
+            moved = jnp.concatenate([before, slab, after, last], axis=0).astype(BF)
+            for b in range(3):
+                to = y + 1 - b
+                if 0 <= to < HY:
+                    x1b[b * 16 : b * 16 + 16, p * CELLS + to * HX : p * CELLS + (to + 1) * HX] = moved
     for p in range(5):
         x3[:, p * ROWS * HX : p * ROWS * HX + HX] = jnp.zeros((96, HX), BF)
-    for p in range(4):
-        pre = bias[0:C_ONE, 0:1]
-        for a in range(3):
-            pre = pre + dot_nn(w1t[a * C_ONE : (a + 1) * C_ONE, :], x1b[:, (p + a) * CELLS : (p + a + 1) * CELLS])
+    pk[384:512, :] = jnp.zeros((128, HX), F32)
+
+    def planes(p):
+        return jnp.concatenate([x1b[:, (p + a) * CELLS : (p + a + 1) * CELLS] for a in range(3)], axis=0)
+
+    def first(p):
+        pre = dot_nn(w1t[...], planes(p)) + bias[0:C_ONE, 0:1]
         sig = sigmoid(pre)
         slope = sig * (1.0 + pre * (1.0 - sig))
         act = pre * sig
@@ -131,65 +135,77 @@
             col = (1 + p * ROWS + y) * HX
             for c, moved in enumerate(neighbours(act[:, y * HX : (y + 1) * HX])):
                 x3[c * C_ONE : (c + 1) * C_ONE, col : col + HX] = moved.astype(BF)
-    for q in range(2):
+
+    def second(q):
         sb[0:C_TWO, q * CELLS + 7 * HX : (q + 1) * CELLS] = jnp.zeros((C_TWO, HX), BF)
         sb[2 * C_TWO :, q * CELLS : q * CELLS + HX] = jnp.zeros((C_TWO, HX), BF)
-        pre = bias[C_ONE:, 0:1]
-        for k in range(9):
-            col = ((q + k // 3) * ROWS + k % 3) * HX
-            pre = pre + dot_nn(w2t[k * C_TWO : (k + 1) * C_TWO, :], x3[:, col : col + CELLS])
-        sig = sigmoid(pre)
-        slope = sig * (1.0 + pre * (1.0 - sig))
-        act = pre * sig
-        for y in range(HY):
-            row = q * HY + y
-            col = row * HX
-            up = cot[:, col : col + HX].astype(F32)
-            here = (up * slope[:, y * HX : (y + 1) * HX]).astype(BF)
-            for b in range(3):
-                to = y + b - 1
-                if 0 <= to < HY:
-                    sb[b * C_TWO : (b + 1) * C_TWO, q * CELLS + to * HX : q * CELLS + (to + 1) * HX] = here
-            for c, moved in enumerate(neighbours(here.astype(F32))):
-                s3[c * C_TWO : (c + 1) * C_TWO, col : col + HX] = moved.astype(BF)
-            fs[pl.ds(row, C_TWO, stride=C_PITCH), :] = act[:, y * HX : (y + 1) * HX]
-    for o in range(C_TWO):
-        for z in range(2):
-            fb[0, o, z] = fs[o * C_PITCH + z * HY : o * C_PITCH + (z + 1) * HY, :].astype(BF)
+        for part in range(0, HY, STEP):
+            cols = [((q + k // 3) * ROWS + k % 3 + part) * HX for k in range(9)]
+            near = jnp.concatenate([x3[:, col : col + STEP * HX] for col in cols], axis=0)
+            pre = dot_nn(w2t[...], near) + bias[C_ONE:, 0:1]
+            sig = sigmoid(pre)
+            slope = sig * (1.0 + pre * (1.0 - sig))
+            act = pre * sig
+            for y in range(part, part + STEP):
+                row = q * HY + y
+                col = row * HX
+                lane = (y - part) * HX
+                up = cot[:, col : col + HX].astype(F32)
+                here = (up * slope[:, lane : lane + HX]).astype(BF)
+                for b in range(3):
+                    to = y + b - 1
+                    if 0 <= to < HY:
+                        sb[b * C_TWO : (b + 1) * C_TWO, q * CELLS + to * HX : q * CELLS + (to + 1) * HX] = here
+                for c, moved in enumerate(neighbours(here.astype(F32))):
+                    s3[c * C_TWO : (c + 1) * C_TWO, col : col + HX] = moved.astype(BF)
+                fs[pl.ds(row, C_TWO, stride=C_PITCH), :] = act[:, lane : lane + HX]
+        for o in range(C_TWO):
+            fb[0, o, q] = fs[o * C_PITCH + q * HY : o * C_PITCH + (q + 1) * HY, :].astype(BF)
+
+    def back(j):
+        rs[:, j * CELLS : (j + 1) * CELLS] = dot_nn(flip[...], s3[:, j * CELLS : (j + 1) * CELLS])
+
+    def two(j):
+        near = [x3[:, (1 + (j + a) * ROWS) * HX : (1 + (j + a) * ROWS) * HX + CELLS] for a in range(3)]
+        near = jnp.concatenate(near + [jnp.ones((16, CELLS), BF)], axis=0)
+        return dot_nt(near, sb[:, j * CELLS : (j + 1) * CELLS])
+
+    first(0)
+    first(1)
+    first(2)
+    first(3)
+    second(0)
+    second(1)
+    back(0)
+    back(1)
+    two_0 = two(0)
+    two_1 = two(1)
     out = pltpu.make_async_copy(fb, features, sem)
     out.start()
-    for j in range(2):
-        rs[:, j * CELLS : (j + 1) * CELLS] = dot_nn(flip[...], s3[:, j * CELLS : (j + 1) * CELLS])
-    pk[384:512, :] = jnp.zeros((128, HX), F32)
-    for a in range(3):
-        grad = 0.0
-        for j in range(2):
-            col = (1 + (j + a) * ROWS) * HX
-            grad = grad + dot_nt(x3[:, col : col + CELLS], sb[:, j * CELLS : (j + 1) * CELLS])
-        for b in range(3):
-            row, lane = place(a * 3 + b)
-            pk[row : row + 96, lane : lane + C_TWO] = grad[:, b * C_TWO : (b + 1) * C_TWO]
-    ones = jnp.ones((8, 2 * CELLS), BF)
-    pk[480:488, 0:C_TWO] = dot_nt(ones, s3[C_TWO : 2 * C_TWO, :])
+    twos = two_0 + two_1
+    for k in range(9):
+        row, lane = place(k)
+        pk[row : row + 96, lane : lane + C_TWO] = twos[k // 3 * 96 : k // 3 * 96 + 96, k % 3 * C_TWO : k % 3 * C_TWO + C_TWO]
+    pk[480:488, C_TWO : 2 * C_TWO] = twos[288:296, C_TWO : 2 * C_TWO]
     grads = 0.0
     for t in range(4):
         shares = []
         for y in range(HY):
-            back = 0.0
+            total = 0.0
             for k in range(9):
                 j, row = t + k // 3 - 2, y + k % 3 - 1
                 if 0 <= j < 2 and 0 <= row < HY:
                     col = j * CELLS + row * HX
-                    back = back + rs[k * C_ONE : (k + 1) * C_ONE, col : col + HX]
-            shares.append(back * p1[:, t * CELLS + y * HX : t * CELLS + (y + 1) * HX])
+                    total = total + rs[k * C_ONE : (k + 1) * C_ONE, col : col + HX]
+            shares.append(total * p1[:, t * CELLS + y * HX : t * CELLS + (y + 1) * HX])
         share = jnp.concatenate(shares, axis=1)
         high = share.astype(BF)
         share = jnp.concatenate([high, (share - high.astype(F32)).astype(BF)], axis=0)
-        near = jnp.concatenate([x1b[:, (t + a) * CELLS : (t + a + 1) * CELLS] for a in range(3)], axis=0)
-        grads = grads + dot_nt(near, share)
+        grads = grads + dot_nt(planes(t), share)
+    grads = grads[:, :C_ONE] + grads[:, C_ONE:]
     for a in range(3):
-        grad = grads[a * 48 : a * 48 + 40]
-        pk[384 + a * 40 : 384 + a * 40 + 40, C_TWO : C_TWO + C_ONE] = grad[:, :C_ONE] + grad[:, C_ONE:]
+        row, lane = place_one(a)
+        pk[row : row + 48, lane : lane + C_ONE] = grads[a * 48 : a * 48 + 48]
     packed[...] = pk[...].astype(BF).reshape(32, 16, HX)
     out.wait()
 
@@ -199,6 +215,10 @@
     if b < 2:
         return a * 96, b * C_TWO
     return (288, a * C_TWO) if a < 2 else (384, 0)
+
+
+def place_one(a):
+    return 384 + a % 2 * 48, C_TWO + a // 2 * C_ONE
 
 
 def unpack(total, two, one, bias_one, bias_two):
@@ -207,11 +227,12 @@
         r, lane = place(k)
         two[3 * k : 3 * k + 3] = flat[r : r + 96, lane : lane + 64].reshape(3, C_ONE, C_TWO)
     for a in range(3):
+        r, lane = place_one(a)
         for t in range(9):
-            r = 384 + a * 40 + t * 4
-            one[a * 9 + t] = flat[r : r + 4, 64:96]
-    bias_one[...] = flat[384 + 36 : 384 + 37, 64:96]
-    bias_two[...] = flat[480:481, 0:64]
+            row = r + t // 3 * 16 + t % 3 * 4
+            one[a * 9 + t] = flat[row : row + 4, lane : lane + C_ONE]
+    bias_one[...] = flat[384 + 12 : 384 + 13, C_TWO : C_TWO + C_ONE]
+    bias_two[...] = flat[480:481, C_TWO : 2 * C_TWO]
 
 
 def exchange(x, axes, first):
@@ -253,8 +274,8 @@
     ready = pl.pallas_call(
         prepare,
         out_shape=(
-            jax.ShapeDtypeStruct((96, 48), BF),
-            jax.ShapeDtypeStruct((576, 96), BF),
+            jax.ShapeDtypeStruct((C_ONE, 144), BF),
+            jax.ShapeDtypeStruct((C_TWO, 864), BF),
             jax.ShapeDtypeStruct((288, 192), BF),
             jax.ShapeDtypeStruct((96, HX), F32),
             jax.ShapeDtypeStruct((C_TWO, 2 * CELLS), BF),
@@ -285,7 +306,6 @@
         out_specs=(HBM, VMEM),
         scratch_shapes=[
             pltpu.VMEM((C_IN * V_PITCH, HX), F32),
-            pltpu.VMEM((48, 6 * CELLS), F32),
             pltpu.VMEM((48, 6 * CELLS), BF),
             pltpu.VMEM((96, 37 * HX), BF),
             pltpu.VMEM((192, 2 * CELLS), BF),

time: 49.5 us -> 48.9 us (0.988)
  Pallas kernels: 6.23 us -> 5.58 us
    pallas_call x1, Pallas kernels: 3.83 us -> 3.22 us  [local(): pl.pallas_call(compute, out_shape=(jax.ShapeDtypeStruct((1, C_TWO, 2, HY,...]
where the time goes in v6:
time: 48.9 us; the launch traced here: 48.7 us
  blocking collectives  39.5 us (81%)
  Pallas kernels  5.58 us (11%)
  starting transfers between devices  2.77 us (6%)
  between operations  0.71 us (1%)
    all_to_all x3, blocking collectives, exchange(): return lax.all_to_all(x, axes, 0, 0, axis_index_groups=[order], tiled=True)  39.5 us
    pallas_call x1, Pallas kernels, local(): pl.pallas_call(compute, out_shape=(jax.ShapeDtypeStruct((1, C_TWO, 2, HY,...  3.22 us
    ppermute x2, starting transfers between devices, swapped(): return lax.ppermute(x, DEPTH, ups + [(j, i) for i, j in ups])  2.77 us
    pallas_call x1, Pallas kernels, local(): pl.pallas_call(prepare, out_shape=(jax.ShapeDtypeStruct((C_ONE, 144), BF)...  1.46 us
  transfers between devices with their start and end apart: 2, of which 0 were waited for; matrix products, arithmetic and copies ran while one was open for 0% of the time, Pallas kernels for 3%

profile of v6, /device:TPU:1, one launch (start us, length us, event | category | flops | bytes accessed | tf_op | source)
XLA Modules:
  0.0 48.7 jit_solution(9369491318261995616)
XLA Ops:
  0.6 2.1 %collective-permute-start = (bf16[1,4,2,8,128]{4,3,2,1,0:T(8,128)(2,1)}, bf16[1,4,2,8,128]{4,3,2,1,0:T(8,128)(2,1)S(1)}, u32[]{:S(2)}, u32[]{:S(2)}) collective-permute-start(bf16[1,4,2,8,128]{4,3,2,1,0:T(8,128)(2,1)} %v0.1), channel_id=1, source_target_pairs={{0,1},{2,3},{4,5},{6,7},{1,0},{3,2},{5,4},{7,6},{8,9},{10,11},{12,... | collective-permute-start | bytes 49160 | tf_op jit(solution)/shard_map/ppermute | solution.py:264
  2.7 0.7 %collective-permute-start.1 = (bf16[1,4,2,8,128]{4,3,2,1,0:T(8,128)(2,1)}, bf16[1,4,2,8,128]{4,3,2,1,0:T(8,128)(2,1)S(1)}, u32[]{:S(2)}, u32[]{:S(2)}) collective-permute-start(bf16[1,4,2,8,128]{4,3,2,1,0:T(8,128)(2,1)} %v0.1), channel_id=1, source_target_pairs={{1,2},{3,4},{5,6},{2,1},{4,3},{6,5},{9,10},{11,12},{13,14},{10,9},... | collective-permute-start | bytes 49160 | tf_op jit(solution)/shard_map/ppermute | solution.py:264
  3.4 0.1 pad_add_fusion.depth
  3.5 0.0 copy-start
  3.5 1.5 %prepare.1 = (bf16[32,144]{1,0:T(8,128)(2,1)S(1)}, bf16[64,864]{1,0:T(8,128)(2,1)S(1)}, bf16[288,192]{1,0:T(8,128)(2,1)S(1)}, f32[96,128]{1,0:T(8,128)S(1)}, bf16[64,2048]{1,0:T(8,128)(2,1)S(1)}) custom-call(bf16[27,4,32]{2,1,0:T(4,128)(2,1)} %bitcast.18, f32[1,32]{1,0:T(1,128)} %bitcast.19, bf16[27,32,64]{2,1,0:T(8,128)(2,1)} %bitcast.17, ...), custom_call_target="tpu_custom_call" | custom-call | tf_op jit(solution)/shard_map/prepare/pallas_call | solution.py:274
  5.0 0.0 collective-permute-done.va
  5.0 0.0 collective-permute-done.1.vb
  5.0 0.0 copy-done
  5.0 3.2 %slab.1 = (bf16[1,64,2,8,128]{4,3,2,1,0:T(8,128)(2,1)}, bf16[32,16,128]{2,1,0:T(8,128)(2,1)S(1)}) custom-call(s32[2]{0:T(128)S(1)} %pad_add_fusion.depth, bf16[1,4,2,8,128]{4,3,2,1,0:T(8,128)(2,1)S(1)} %collective-permute-done.va, bf16[1,4,2,8,128]{4,3,2,1,0:T(8,128)(2,1)S(1)} %copy-done, bf16[1,4,2,8,128]{4,3,2,1,0:T(8,128)(2,1)S(1)} %collective-permute-done.1.vb, ...), custom_call_target="tpu_custom_call" | custom-call | tf_op jit(solution)/shard_map/slab/pallas_call | solution.py:299
  8.2 15.9 %all_to_all.15 = bf16[32,16,128]{2,1,0:T(8,128)(2,1)S(1)} all-to-all(bf16[32,16,128]{2,1,0:T(8,128)(2,1)S(1)} %get-tuple-element.22), channel_id=1, replica_groups={{28,0,1,2,3,4,5,6,7,8,9,10,11,12,13,14,15,16,17,18,19,20,21,22,23,24,25..., dimensions={0} | all-to-all | bytes 262144 | tf_op jit(solution)/shard_map/all_to_all | solution.py:240
  24.2 11.5 %all_to_all.16 = bf16[8,16,128]{2,1,0:T(8,128)(2,1)S(1)} all-to-all(bf16[8,16,128]{2,1,0:T(8,128)(2,1)S(1)} %broadcast_in_dim.20), channel_id=1, replica_groups={{128,0,32,64,96,160,192,224},{129,1,33,65,97,161,193,225},{130,2,34,66,..., dimensions={0} | all-to-all | bytes 65536 | tf_op jit(solution)/shard_map/all_to_all | solution.py:240
  35.7 12.1 %all_to_all.17.total = bf16[32,16,128]{2,1,0:T(8,128)(2,1)S(1)} all-to-all(bf16[32,16,128]{2,1,0:T(8,128)(2,1)S(1)} %broadcast_in_dim.21), channel_id=1, replica_groups={{28,0,1,2,3,4,5,6,7,8,9,10,11,12,13,14,15,16,17,18,19,20,21,22,23,24,25..., dimensions={0} | all-to-all | bytes 262144 | tf_op jit(solution)/shard_map/all_to_all | solution.py:240
  47.8 0.9 %unpack.1 = (f32[27,32,64]{2,1,0:T(8,128)}, f32[27,4,32]{2,1,0:T(4,128)}, f32[1,32]{1,0:T(1,128)}, f32[1,64]{1,0:T(1,128)}) custom-call(bf16[32,16,128]{2,1,0:T(8,128)(2,1)S(1)} %all_to_all.17.total), custom_call_target="tpu_custom_call" | custom-call | tf_op jit(solution)/shard_map/unpack/pallas_call | solution.py:327
  (4 shorter events, 0.1 us)
Async XLA Ops:
  0.6 4.3 %collective-permute-start = (bf16[1,4,2,8,128]{4,3,2,1,0:T(8,128)(2,1)}, bf16[1,4,2,8,128]{4,3,2,1,0:T(8,128)(2,1)S(1)}, u32[]{:S(2)}, u32[]{:S(2)}) collective-permute-start(bf16[1,4,2,8,128]{4,3,2,1,0:T(8,128)(2,1)} %v0.1), channel_id=1, source_target_pairs={{0,1},{2,3},{4,5},{6,7},{1,0},{3,2},{5,4},{7,6},{8,9},{10,11},{12,... | collective-permute-start | bytes 49160 | tf_op jit(solution)/shard_map/ppermute | solution.py:264
  2.7 2.2 %collective-permute-start.1 = (bf16[1,4,2,8,128]{4,3,2,1,0:T(8,128)(2,1)}, bf16[1,4,2,8,128]{4,3,2,1,0:T(8,128)(2,1)S(1)}, u32[]{:S(2)}, u32[]{:S(2)}) collective-permute-start(bf16[1,4,2,8,128]{4,3,2,1,0:T(8,128)(2,1)} %v0.1), channel_id=1, source_target_pairs={{1,2},{3,4},{5,6},{2,1},{4,3},{6,5},{9,10},{11,12},{13,14},{10,9},... | collective-permute-start | bytes 49160 | tf_op jit(solution)/shard_map/ppermute | solution.py:264
  3.5 1.5 %copy-start = (bf16[1,4,2,8,128]{4,3,2,1,0:T(8,128)(2,1)S(1)}, bf16[1,4,2,8,128]{4,3,2,1,0:T(8,128)(2,1)}, u32[]{:S(2)}) copy-start(bf16[1,4,2,8,128]{4,3,2,1,0:T(8,128)(2,1)} %v0.1) | copy-start | bytes 49156

commit v7 on v6

--- a/solution.py
+++ b/solution.py
@@ -52,15 +52,34 @@
 
 def neighbours(x):
     lane = lax.broadcasted_iota(jnp.int32, x.shape, 1)
-    before = jnp.where(lane == 0, 0.0, pltpu.roll(x, 1, 1))
-    after = jnp.where(lane == HX - 1, 0.0, pltpu.roll(x, HX - 1, 1))
+    zero = jnp.zeros((), x.dtype)
+    before = jnp.where(lane == 0, zero, pltpu.roll(x, 1, 1))
+    after = jnp.where(lane == HX - 1, zero, pltpu.roll(x, HX - 1, 1))
     return before, x, after
 
 
-def prepare(w1, b1, w2, b2, c0, w1t, w2t, flip, bias, cot, w1v, w2v, cv, bv1, bv2, w1s, cs, sems):
+def taps(to, p, load):
+    last = jnp.where(lax.broadcasted_iota(jnp.int32, (4, HX), 0) == 0, 1.0, 0.0)
+    edge = jnp.concatenate([jnp.zeros((12, HX), F32), last], axis=0).astype(BF)
+    to[0:16, p * CELLS : p * CELLS + HX] = edge
+    to[32:48, p * CELLS + 7 * HX : (p + 1) * CELLS] = edge
+    for y in range(HY):
+        before, slab, after = neighbours(load(y))
+        moved = jnp.concatenate([before, slab, after, last], axis=0).astype(BF)
+        for b in range(3):
+            row = y + 1 - b
+            if 0 <= row < HY:
+                to[b * 16 : b * 16 + 16, p * CELLS + row * HX : p * CELLS + (row + 1) * HX] = moved
+
+
+def prepare(
+    v0, w1, b1, w2, b2, c0,
+    own, w1t, w2t, flip, bias, cot,
+    vv, w1v, w2v, cv, bv1, bv2, vs, w1s, cs, sems,
+):
     copies = [
         pltpu.make_async_copy(src, dst, sems.at[n])
-        for n, (src, dst) in enumerate(((w1, w1v), (w2, w2v), (b1, bv1), (b2, bv2), (c0, cv)))
+        for n, (src, dst) in enumerate(((w1, w1v), (w2, w2v), (b1, bv1), (b2, bv2), (c0, cv), (v0, vv)))
     ]
     for copy in copies:
         copy.start()
@@ -79,6 +98,12 @@
     copies[3].wait()
     bias[0:C_ONE, :] = jnp.broadcast_to(column(bv1[...]), (C_ONE, HX))
     bias[C_ONE:, :] = jnp.broadcast_to(column(bv2[...]), (C_TWO, HX))
+    copies[5].wait()
+    for p in range(2):
+        for i in range(C_IN):
+            vs[i * V_PITCH + p * HY : i * V_PITCH + (p + 1) * HY, :] = vv[0, i, p].astype(F32)
+    for p in range(2):
+        taps(own, p, lambda y: vs[pl.ds(p * HY + y, C_IN, stride=V_PITCH), :])
     copies[4].wait()
     for o in range(C_TWO):
         for z in range(2):
@@ -88,44 +113,34 @@
 
 
 def compute(
-    depth, va, v0, vb, w1t, w2t, flip, bias, cot,
+    depth, va, vb, own, w1t, w2t, flip, bias, cot,
     features, packed,
-    vs, x1b, x3, s3, sb, fs, fb, p1, rs, pk, sem,
+    vs, x1b, x3, s3, sb, fs, fb, p1, rs, sem,
 ):
-    even = depth[0] % 2 == 0
-    for p in range(6):
+    even = depth[0] % 2 == 1
+    for p in range(4):
         for i in range(C_IN):
-            if p in (2, 3):
-                plane = v0[0, i, p % 2].astype(F32)
-            else:
-                near = va[0, i, p % 2].astype(F32)
-                far = vb[0, i, p % 2].astype(F32)
-                plane = jnp.where(even, far, near) if p < 2 else jnp.where(even, near, far)
+            near = va[0, i, p % 2].astype(F32)
+            far = vb[0, i, p % 2].astype(F32)
+            plane = jnp.where(even, far, near) if p < 2 else jnp.where(even, near, far)
             vs[i * V_PITCH + p * HY : i * V_PITCH + (p + 1) * HY, :] = plane
-    last = jnp.where(lax.broadcasted_iota(jnp.int32, (4, HX), 0) == 0, 1.0, 0.0)
-    edge = jnp.concatenate([jnp.zeros((12, HX), F32), last], axis=0).astype(BF)
-    for p in range(6):
-        x1b[0:16, p * CELLS : p * CELLS + HX] = edge
-        x1b[32:48, p * CELLS + 7 * HX : (p + 1) * CELLS] = edge
-        for y in range(HY):
-            before, slab, after = neighbours(vs[pl.ds(p * HY + y, C_IN, stride=V_PITCH), :])
-            moved = jnp.concatenate([before, slab, after, last], axis=0).astype(BF)
-            for b in range(3):
-                to = y + 1 - b
-                if 0 <= to < HY:
-                    x1b[b * 16 : b * 16 + 16, p * CELLS + to * HX : p * CELLS + (to + 1) * HX] = moved
+    for p in range(4):
+        taps(x1b, p, lambda y: vs[pl.ds(p * HY + y, C_IN, stride=V_PITCH), :])
     for p in range(5):
         x3[:, p * ROWS * HX : p * ROWS * HX + HX] = jnp.zeros((96, HX), BF)
-    pk[384:512, :] = jnp.zeros((128, HX), F32)
 
     def planes(p):
-        return jnp.concatenate([x1b[:, (p + a) * CELLS : (p + a + 1) * CELLS] for a in range(3)], axis=0)
+        parts = []
+        for q in (p, p + 1, p + 2):
+            ref, at = (own, q - 2) if q in (2, 3) else (x1b, q if q < 2 else q - 2)
+            parts.append(ref[:, at * CELLS : (at + 1) * CELLS])
+        return jnp.concatenate(parts, axis=0)
 
     def first(p):
         pre = dot_nn(w1t[...], planes(p)) + bias[0:C_ONE, 0:1]
         sig = sigmoid(pre)
-        slope = sig * (1.0 + pre * (1.0 - sig))
         act = pre * sig
+        slope = sig + act * (1.0 - sig)
         if p in (0, 3):
             inside = jnp.where(depth[0] > 0 if p == 0 else depth[0] < depth[1] - 1, 1.0, 0.0)
             slope = slope * inside
@@ -133,8 +148,8 @@
         p1[:, p * CELLS : (p + 1) * CELLS] = slope
         for y in range(HY):
             col = (1 + p * ROWS + y) * HX
-            for c, moved in enumerate(neighbours(act[:, y * HX : (y + 1) * HX])):
-                x3[c * C_ONE : (c + 1) * C_ONE, col : col + HX] = moved.astype(BF)
+            for c, moved in enumerate(neighbours(act[:, y * HX : (y + 1) * HX].astype(BF))):
+                x3[c * C_ONE : (c + 1) * C_ONE, col : col + HX] = moved
 
     def second(q):
         sb[0:C_TWO, q * CELLS + 7 * HX : (q + 1) * CELLS] = jnp.zeros((C_TWO, HX), BF)
@@ -144,8 +159,8 @@
             near = jnp.concatenate([x3[:, col : col + STEP * HX] for col in cols], axis=0)
             pre = dot_nn(w2t[...], near) + bias[C_ONE:, 0:1]
             sig = sigmoid(pre)
-            slope = sig * (1.0 + pre * (1.0 - sig))
             act = pre * sig
+            slope = sig + act * (1.0 - sig)
             for y in range(part, part + STEP):
                 row = q * HY + y
                 col = row * HX
@@ -156,8 +171,8 @@
                     to = y + b - 1
                     if 0 <= to < HY:
                         sb[b * C_TWO : (b + 1) * C_TWO, q * CELLS + to * HX : q * CELLS + (to + 1) * HX] = here
-                for c, moved in enumerate(neighbours(here.astype(F32))):
-                    s3[c * C_TWO : (c + 1) * C_TWO, col : col + HX] = moved.astype(BF)
+                for c, moved in enumerate(neighbours(here)):
+                    s3[c * C_TWO : (c + 1) * C_TWO, col : col + HX] = moved
                 fs[pl.ds(row, C_TWO, stride=C_PITCH), :] = act[:, lane : lane + HX]
         for o in range(C_TWO):
             fb[0, o, q] = fs[o * C_PITCH + q * HY : o * C_PITCH + (q + 1) * HY, :].astype(BF)
@@ -183,10 +198,6 @@
     out = pltpu.make_async_copy(fb, features, sem)
     out.start()
     twos = two_0 + two_1
-    for k in range(9):
-        row, lane = place(k)
-        pk[row : row + 96, lane : lane + C_TWO] = twos[k // 3 * 96 : k // 3 * 96 + 96, k % 3 * C_TWO : k % 3 * C_TWO + C_TWO]
-    pk[480:488, C_TWO : 2 * C_TWO] = twos[288:296, C_TWO : 2 * C_TWO]
     grads = 0.0
     for t in range(4):
         shares = []
@@ -203,10 +214,19 @@
         share = jnp.concatenate([high, (share - high.astype(F32)).astype(BF)], axis=0)
         grads = grads + dot_nt(planes(t), share)
     grads = grads[:, :C_ONE] + grads[:, C_ONE:]
-    for a in range(3):
-        row, lane = place_one(a)
-        pk[row : row + 48, lane : lane + C_ONE] = grads[a * 48 : a * 48 + 48]
-    packed[...] = pk[...].astype(BF).reshape(32, 16, HX)
+    side = twos[:, 2 * C_TWO :]
+    third = jnp.concatenate([grads[96:], jnp.zeros((48, C_ONE), F32)], axis=0)
+    rows = jnp.concatenate(
+        [
+            twos[:288, : 2 * C_TWO],
+            jnp.concatenate([side[:96], side[96:192]], axis=1),
+            jnp.concatenate([side[192:288], grads[:96], third], axis=1),
+            twos[288:, : 2 * C_TWO],
+            jnp.zeros((16, HX), F32),
+        ],
+        axis=0,
+    )
+    packed[...] = rows.astype(BF).reshape(32, 16, HX)
     out.wait()
 
 
@@ -269,28 +289,31 @@
 SMEM = pl.BlockSpec(memory_space=pltpu.SMEM)
 
 
-def local(depth, volumes, w1, b1, w2, b2, cot, interpret=False):
-    held = [x if interpret else pltpu.with_memory_space_constraint(x, pltpu.HBM) for x in (w1, b1, w2, b2, cot)]
+def local(depth, va, v0, vb, w1, b1, w2, b2, cot, interpret=False):
+    held = [x if interpret else pltpu.with_memory_space_constraint(x, pltpu.HBM) for x in (v0, w1, b1, w2, b2, cot)]
     ready = pl.pallas_call(
         prepare,
         out_shape=(
+            jax.ShapeDtypeStruct((48, 2 * CELLS), BF),
             jax.ShapeDtypeStruct((C_ONE, 144), BF),
             jax.ShapeDtypeStruct((C_TWO, 864), BF),
             jax.ShapeDtypeStruct((288, 192), BF),
             jax.ShapeDtypeStruct((96, HX), F32),
             jax.ShapeDtypeStruct((C_TWO, 2 * CELLS), BF),
         ),
-        in_specs=[HBM] * 5,
-        out_specs=(VMEM,) * 5,
+        in_specs=[HBM] * 6,
+        out_specs=(VMEM,) * 6,
         scratch_shapes=[
+            pltpu.VMEM((1, C_IN, 2, HY, HX), BF),
             pltpu.VMEM((27, C_IN, C_ONE), BF),
             pltpu.VMEM((27, C_ONE, C_TWO), BF),
             pltpu.VMEM((1, C_TWO, 2, HY, HX), BF),
             pltpu.VMEM((1, C_ONE), F32),
             pltpu.VMEM((1, C_TWO), F32),
+            pltpu.VMEM((C_IN * V_PITCH, HX), F32),
             pltpu.VMEM((144, C_ONE), F32),
             pltpu.VMEM((C_TWO * C_PITCH, HX), F32),
-            pltpu.SemaphoreType.DMA((5,)),
+            pltpu.SemaphoreType.DMA((6,)),
         ],
         compiler_params=pltpu.CompilerParams(vmem_limit_bytes=16 * 1024 * 1024),
         interpret=interpret,
@@ -306,7 +329,7 @@
         out_specs=(HBM, VMEM),
         scratch_shapes=[
             pltpu.VMEM((C_IN * V_PITCH, HX), F32),
-            pltpu.VMEM((48, 6 * CELLS), BF),
+            pltpu.VMEM((48, 4 * CELLS), BF),
             pltpu.VMEM((96, 37 * HX), BF),
             pltpu.VMEM((192, 2 * CELLS), BF),
             pltpu.VMEM((192, 2 * CELLS), BF),
@@ -314,13 +337,12 @@
             pltpu.VMEM((1, C_TWO, 2, HY, HX), BF),
             pltpu.VMEM((C_ONE, 4 * CELLS), F32),
             pltpu.VMEM((288, 2 * CELLS), F32),
-            pltpu.VMEM((512, HX), F32),
             pltpu.SemaphoreType.DMA,
         ],
         compiler_params=pltpu.CompilerParams(vmem_limit_bytes=24 * 1024 * 1024),
         interpret=interpret,
         name="slab",
-    )(depth, *volumes, *ready)
+    )(depth, va, vb, *ready)
 
 
 def split(total, interpret=False):
@@ -341,11 +363,11 @@
 
 
 def per_device(volume, kernel_one, bias_one, kernel_two, bias_two, cotangent):
-    volumes = (swapped(volume, 0), volume, swapped(volume, 1))
+    even, odd = swapped(volume, 0), swapped(volume, 1)
     depth = jnp.stack([lax.axis_index(DEPTH), lax.axis_size(DEPTH)]).astype(jnp.int32)
     w1 = jnp.transpose(kernel_one, (2, 3, 4, 1, 0)).reshape(27, C_IN, C_ONE)
     w2 = jnp.transpose(kernel_two, (2, 3, 4, 1, 0)).reshape(27, C_ONE, C_TWO)
-    features, packed = local(depth, volumes, w1, bias_one[None], w2, bias_two[None], cotangent)
+    features, packed = local(depth, odd, volume, even, w1, bias_one[None], w2, bias_two[None], cotangent)
     two, one, b1, b2 = split(reduced(packed))
     two = jnp.transpose(two.reshape(3, 3, 3, C_ONE, C_TWO), (4, 3, 0, 1, 2))
     one = jnp.transpose(one.reshape(3, 3, 3, C_IN, C_ONE), (4, 3, 0, 1, 2))

time: 48.9 us -> 48.1 us (0.984)
  blocking collectives: 39.5 us -> 36.2 us
  starting transfers between devices: 2.77 us -> 5.29 us
    all_to_all x3, blocking collectives: 39.5 us -> 36.2 us  [exchange(): return lax.all_to_all(x, axes, 0, 0, axis_index_groups=[order], tiled=True)]
    ppermute x2, starting transfers between devices: 2.77 us -> 5.29 us  [swapped(): return lax.ppermute(x, DEPTH, ups + [(j, i) for i, j in ups])]
where the time goes in v7:
time: 48.1 us; the launch traced here: 47.8 us
  blocking collectives  36.2 us (75%)
  Pallas kernels  5.48 us (11%)
  starting transfers between devices  5.29 us (11%)
  between operations  0.69 us (1%)
    all_to_all x3, blocking collectives, exchange(): return lax.all_to_all(x, axes, 0, 0, axis_index_groups=[order], tiled=True)  36.2 us
    ppermute x2, starting transfers between devices, swapped(): return lax.ppermute(x, DEPTH, ups + [(j, i) for i, j in ups])  5.29 us
    pallas_call x1, Pallas kernels, local(): pl.pallas_call(compute, out_shape=(jax.ShapeDtypeStruct((1, C_TWO, 2, HY,...  3.03 us
    pallas_call x1, Pallas kernels, local(): pl.pallas_call(prepare, out_shape=(jax.ShapeDtypeStruct((48, 2 * CELLS),...  1.57 us
  transfers between devices with their start and end apart: 2, of which 0 were waited for; matrix products, arithmetic and copies ran while one was open for 0% of the time, Pallas kernels for 3%

profile of v7, /device:TPU:1, one launch (start us, length us, event | category | flops | bytes accessed | tf_op | source)
XLA Modules:
  0.0 47.8 jit_solution(1662661803102366591)
XLA Ops:
  0.6 0.7 %collective-permute-start = (bf16[1,4,2,8,128]{4,3,2,1,0:T(8,128)(2,1)}, bf16[1,4,2,8,128]{4,3,2,1,0:T(8,128)(2,1)S(1)}, u32[]{:S(2)}, u32[]{:S(2)}) collective-permute-start(bf16[1,4,2,8,128]{4,3,2,1,0:T(8,128)(2,1)} %v0.1), channel_id=1, source_target_pairs={{1,2},{3,4},{5,6},{2,1},{4,3},{6,5},{9,10},{11,12},{13,14},{10,9},... | collective-permute-start | bytes 49160 | tf_op jit(solution)/shard_map/ppermute | solution.py:284
  1.3 4.6 %collective-permute-start.1 = (bf16[1,4,2,8,128]{4,3,2,1,0:T(8,128)(2,1)}, bf16[1,4,2,8,128]{4,3,2,1,0:T(8,128)(2,1)S(1)}, u32[]{:S(2)}, u32[]{:S(2)}) collective-permute-start(bf16[1,4,2,8,128]{4,3,2,1,0:T(8,128)(2,1)} %v0.1), channel_id=1, source_target_pairs={{0,1},{2,3},{4,5},{6,7},{1,0},{3,2},{5,4},{7,6},{8,9},{10,11},{12,... | collective-permute-start | bytes 49160 | tf_op jit(solution)/shard_map/ppermute | solution.py:284
  5.9 0.1 pad_add_fusion.depth
  6.0 1.6 %prepare.1 = (bf16[48,2048]{1,0:T(8,128)(2,1)S(1)}, bf16[32,144]{1,0:T(8,128)(2,1)S(1)}, bf16[64,864]{1,0:T(8,128)(2,1)S(1)}, bf16[288,192]{1,0:T(8,128)(2,1)S(1...) custom-call(bf16[1,4,2,8,128]{4,3,2,1,0:T(8,128)(2,1)} %v0.1, bf16[27,4,32]{2,1,0:T(4,128)(2,1)} %bitcast.18, ...), custom_call_target="tpu_custom_call" | custom-call | tf_op jit(solution)/shard_map/prepare/pallas_call | solution.py:294
  7.6 0.0 collective-permute-done.va
  7.6 0.0 collective-permute-done.1.vb
  7.6 3.0 %slab.1 = (bf16[1,64,2,8,128]{4,3,2,1,0:T(8,128)(2,1)}, bf16[32,16,128]{2,1,0:T(8,128)(2,1)S(1)}) custom-call(s32[2]{0:T(128)S(1)} %pad_add_fusion.depth, bf16[1,4,2,8,128]{4,3,2,1,0:T(8,128)(2,1)S(1)} %collective-permute-done.va, bf16[1,4,2,8,128]{4,3,2,1,0:T(8,128)(2,1)S(1)} %collective-permute-done.1.vb, bf16[48,2048]{1,0:T(8,128)(2,1)S(1)} %get-tuple-element.17.own, ...), custom_call_target="tpu_custom_call" | custom-call | tf_op jit(solution)/shard_map/slab/pallas_call | solution.py:322
  10.6 12.6 %all_to_all.15 = bf16[32,16,128]{2,1,0:T(8,128)(2,1)S(1)} all-to-all(bf16[32,16,128]{2,1,0:T(8,128)(2,1)S(1)} %get-tuple-element.24), channel_id=1, replica_groups={{28,0,1,2,3,4,5,6,7,8,9,10,11,12,13,14,15,16,17,18,19,20,21,22,23,24,25..., dimensions={0} | all-to-all | bytes 262144 | tf_op jit(solution)/shard_map/all_to_all | solution.py:260
  23.3 11.5 %all_to_all.16 = bf16[8,16,128]{2,1,0:T(8,128)(2,1)S(1)} all-to-all(bf16[8,16,128]{2,1,0:T(8,128)(2,1)S(1)} %broadcast_in_dim.20), channel_id=1, replica_groups={{128,0,32,64,96,160,192,224},{129,1,33,65,97,161,193,225},{130,2,34,66,..., dimensions={0} | all-to-all | bytes 65536 | tf_op jit(solution)/shard_map/all_to_all | solution.py:260
  34.9 12.1 %all_to_all.17.total = bf16[32,16,128]{2,1,0:T(8,128)(2,1)S(1)} all-to-all(bf16[32,16,128]{2,1,0:T(8,128)(2,1)S(1)} %broadcast_in_dim.21), channel_id=1, replica_groups={{28,0,1,2,3,4,5,6,7,8,9,10,11,12,13,14,15,16,17,18,19,20,21,22,23,24,25..., dimensions={0} | all-to-all | bytes 262144 | tf_op jit(solution)/shard_map/all_to_all | solution.py:260
  46.9 0.9 %unpack.1 = (f32[27,32,64]{2,1,0:T(8,128)}, f32[27,4,32]{2,1,0:T(4,128)}, f32[1,32]{1,0:T(1,128)}, f32[1,64]{1,0:T(1,128)}) custom-call(bf16[32,16,128]{2,1,0:T(8,128)(2,1)S(1)} %all_to_all.17.total), custom_call_target="tpu_custom_call" | custom-call | tf_op jit(solution)/shard_map/unpack/pallas_call | solution.py:349
  (4 shorter events, 0.1 us)
Async XLA Ops:
  0.6 7.0 %collective-permute-start = (bf16[1,4,2,8,128]{4,3,2,1,0:T(8,128)(2,1)}, bf16[1,4,2,8,128]{4,3,2,1,0:T(8,128)(2,1)S(1)}, u32[]{:S(2)}, u32[]{:S(2)}) collective-permute-start(bf16[1,4,2,8,128]{4,3,2,1,0:T(8,128)(2,1)} %v0.1), channel_id=1, source_target_pairs={{1,2},{3,4},{5,6},{2,1},{4,3},{6,5},{9,10},{11,12},{13,14},{10,9},... | collective-permute-start | bytes 49160 | tf_op jit(solution)/shard_map/ppermute | solution.py:284
  1.3 6.3 %collective-permute-start.1 = (bf16[1,4,2,8,128]{4,3,2,1,0:T(8,128)(2,1)}, bf16[1,4,2,8,128]{4,3,2,1,0:T(8,128)(2,1)S(1)}, u32[]{:S(2)}, u32[]{:S(2)}) collective-permute-start(bf16[1,4,2,8,128]{4,3,2,1,0:T(8,128)(2,1)} %v0.1), channel_id=1, source_target_pairs={{0,1},{2,3},{4,5},{6,7},{1,0},{3,2},{5,4},{7,6},{8,9},{10,11},{12,... | collective-permute-start | bytes 49160 | tf_op jit(solution)/shard_map/ppermute | solution.py:284

commit v8 on v7

--- a/solution.py
+++ b/solution.py
@@ -241,11 +241,16 @@
     return 384 + a % 2 * 48, C_TWO + a // 2 * C_ONE
 
 
-def unpack(total, two, one, bias_one, bias_two):
+def unpack(total, out, one, bias_one, bias_two, two, sems):
     flat = total[...].astype(F32).reshape(512, HX)
+    copies = []
     for k in range(9):
         r, lane = place(k)
         two[3 * k : 3 * k + 3] = flat[r : r + 96, lane : lane + 64].reshape(3, C_ONE, C_TWO)
+        if k % 3 == 2:
+            part = pl.ds(9 * (k // 3), 9)
+            copies.append(pltpu.make_async_copy(two.at[part], out.at[part], sems.at[k // 3]))
+            copies[-1].start()
     for a in range(3):
         r, lane = place_one(a)
         for t in range(9):
@@ -253,6 +258,8 @@
             one[a * 9 + t] = flat[row : row + 4, lane : lane + C_ONE]
     bias_one[...] = flat[384 + 12 : 384 + 13, C_TWO : C_TWO + C_ONE]
     bias_two[...] = flat[480:481, C_TWO : 2 * C_TWO]
+    for copy in copies:
+        copy.wait()
 
 
 def exchange(x, axes, first):
@@ -355,7 +362,8 @@
             jax.ShapeDtypeStruct((1, C_TWO), F32),
         ),
         in_specs=[VMEM],
-        out_specs=(VMEM,) * 4,
+        out_specs=(HBM, VMEM, VMEM, VMEM),
+        scratch_shapes=[pltpu.VMEM((27, C_ONE, C_TWO), F32), pltpu.SemaphoreType.DMA((3,))],
         compiler_params=pltpu.CompilerParams(vmem_limit_bytes=4 * 1024 * 1024),
         interpret=interpret,
         name="unpack",

time: 48.1 us -> 48.7 us (1.012)
  Pallas kernels: 5.48 us -> 6.08 us
    pallas_call x1, Pallas kernels: 0.89 us -> 1.49 us  [split(): pl.pallas_call(unpack, out_shape=(jax.ShapeDtypeStruct((27, C_ONE, C_TWO)...]
where the time goes in v8:
time: 48.7 us; the launch traced here: 48.4 us
  blocking collectives  36.2 us (74%)
  Pallas kernels  6.08 us (12%)
  starting transfers between devices  5.29 us (11%)
  between operations  0.69 us (1%)
    all_to_all x3, blocking collectives, exchange(): return lax.all_to_all(x, axes, 0, 0, axis_index_groups=[order], tiled=True)  36.2 us
    ppermute x2, starting transfers between devices, swapped(): return lax.ppermute(x, DEPTH, ups + [(j, i) for i, j in ups])  5.29 us
    pallas_call x1, Pallas kernels, local(): pl.pallas_call(compute, out_shape=(jax.ShapeDtypeStruct((1, C_TWO, 2, HY,...  3.03 us
    pallas_call x1, Pallas kernels, local(): pl.pallas_call(prepare, out_shape=(jax.ShapeDtypeStruct((48, 2 * CELLS),...  1.57 us
    pallas_call x1, Pallas kernels, split(): pl.pallas_call(unpack, out_shape=(jax.ShapeDtypeStruct((27, C_ONE, C_TWO)...  1.49 us
  transfers between devices with their start and end apart: 2, of which 0 were waited for; matrix products, arithmetic and copies ran while one was open for 0% of the time, Pallas kernels for 3%

profile of v8, /device:TPU:1, one launch (start us, length us, event | category | flops | bytes accessed | tf_op | source)
XLA Modules:
  0.0 48.4 jit_solution(1792876040898054642)
XLA Ops:
  0.6 0.7 %collective-permute-start = (bf16[1,4,2,8,128]{4,3,2,1,0:T(8,128)(2,1)}, bf16[1,4,2,8,128]{4,3,2,1,0:T(8,128)(2,1)S(1)}, u32[]{:S(2)}, u32[]{:S(2)}) collective-permute-start(bf16[1,4,2,8,128]{4,3,2,1,0:T(8,128)(2,1)} %v0.1), channel_id=1, source_target_pairs={{1,2},{3,4},{5,6},{2,1},{4,3},{6,5},{9,10},{11,12},{13,14},{10,9},... | collective-permute-start | bytes 49160 | tf_op jit(solution)/shard_map/ppermute | solution.py:291
  1.3 4.6 %collective-permute-start.1 = (bf16[1,4,2,8,128]{4,3,2,1,0:T(8,128)(2,1)}, bf16[1,4,2,8,128]{4,3,2,1,0:T(8,128)(2,1)S(1)}, u32[]{:S(2)}, u32[]{:S(2)}) collective-permute-start(bf16[1,4,2,8,128]{4,3,2,1,0:T(8,128)(2,1)} %v0.1), channel_id=1, source_target_pairs={{0,1},{2,3},{4,5},{6,7},{1,0},{3,2},{5,4},{7,6},{8,9},{10,11},{12,... | collective-permute-start | bytes 49160 | tf_op jit(solution)/shard_map/ppermute | solution.py:291
  5.9 0.1 pad_add_fusion.depth
  6.0 1.6 %prepare.1 = (bf16[48,2048]{1,0:T(8,128)(2,1)S(1)}, bf16[32,144]{1,0:T(8,128)(2,1)S(1)}, bf16[64,864]{1,0:T(8,128)(2,1)S(1)}, bf16[288,192]{1,0:T(8,128)(2,1)S(1...) custom-call(bf16[1,4,2,8,128]{4,3,2,1,0:T(8,128)(2,1)} %v0.1, bf16[27,4,32]{2,1,0:T(4,128)(2,1)} %bitcast.18, ...), custom_call_target="tpu_custom_call" | custom-call | tf_op jit(solution)/shard_map/prepare/pallas_call | solution.py:301
  7.6 0.0 collective-permute-done.va
  7.6 0.0 collective-permute-done.1.vb
  7.6 3.0 %slab.1 = (bf16[1,64,2,8,128]{4,3,2,1,0:T(8,128)(2,1)}, bf16[32,16,128]{2,1,0:T(8,128)(2,1)S(1)}) custom-call(s32[2]{0:T(128)S(1)} %pad_add_fusion.depth, bf16[1,4,2,8,128]{4,3,2,1,0:T(8,128)(2,1)S(1)} %collective-permute-done.va, bf16[1,4,2,8,128]{4,3,2,1,0:T(8,128)(2,1)S(1)} %collective-permute-done.1.vb, bf16[48,2048]{1,0:T(8,128)(2,1)S(1)} %get-tuple-element.17.own, ...), custom_call_target="tpu_custom_call" | custom-call | tf_op jit(solution)/shard_map/slab/pallas_call | solution.py:329
  10.6 12.6 %all_to_all.15 = bf16[32,16,128]{2,1,0:T(8,128)(2,1)S(1)} all-to-all(bf16[32,16,128]{2,1,0:T(8,128)(2,1)S(1)} %get-tuple-element.24), channel_id=1, replica_groups={{28,0,1,2,3,4,5,6,7,8,9,10,11,12,13,14,15,16,17,18,19,20,21,22,23,24,25..., dimensions={0} | all-to-all | bytes 262144 | tf_op jit(solution)/shard_map/all_to_all | solution.py:267
  23.3 11.5 %all_to_all.16 = bf16[8,16,128]{2,1,0:T(8,128)(2,1)S(1)} all-to-all(bf16[8,16,128]{2,1,0:T(8,128)(2,1)S(1)} %broadcast_in_dim.20), channel_id=1, replica_groups={{128,0,32,64,96,160,192,224},{129,1,33,65,97,161,193,225},{130,2,34,66,..., dimensions={0} | all-to-all | bytes 65536 | tf_op jit(solution)/shard_map/all_to_all | solution.py:267
  34.9 12.1 %all_to_all.17.total = bf16[32,16,128]{2,1,0:T(8,128)(2,1)S(1)} all-to-all(bf16[32,16,128]{2,1,0:T(8,128)(2,1)S(1)} %broadcast_in_dim.21), channel_id=1, replica_groups={{28,0,1,2,3,4,5,6,7,8,9,10,11,12,13,14,15,16,17,18,19,20,21,22,23,24,25..., dimensions={0} | all-to-all | bytes 262144 | tf_op jit(solution)/shard_map/all_to_all | solution.py:267
  46.9 1.5 %unpack.1 = (f32[27,32,64]{2,1,0:T(8,128)}, f32[27,4,32]{2,1,0:T(4,128)}, f32[1,32]{1,0:T(1,128)}, f32[1,64]{1,0:T(1,128)}) custom-call(bf16[32,16,128]{2,1,0:T(8,128)(2,1)S(1)} %all_to_all.17.total), custom_call_target="tpu_custom_call" | custom-call | tf_op jit(solution)/shard_map/unpack/pallas_call | solution.py:356
  (4 shorter events, 0.1 us)
Async XLA Ops:
  0.6 7.0 %collective-permute-start = (bf16[1,4,2,8,128]{4,3,2,1,0:T(8,128)(2,1)}, bf16[1,4,2,8,128]{4,3,2,1,0:T(8,128)(2,1)S(1)}, u32[]{:S(2)}, u32[]{:S(2)}) collective-permute-start(bf16[1,4,2,8,128]{4,3,2,1,0:T(8,128)(2,1)} %v0.1), channel_id=1, source_target_pairs={{1,2},{3,4},{5,6},{2,1},{4,3},{6,5},{9,10},{11,12},{13,14},{10,9},... | collective-permute-start | bytes 49160 | tf_op jit(solution)/shard_map/ppermute | solution.py:291
  1.3 6.3 %collective-permute-start.1 = (bf16[1,4,2,8,128]{4,3,2,1,0:T(8,128)(2,1)}, bf16[1,4,2,8,128]{4,3,2,1,0:T(8,128)(2,1)S(1)}, u32[]{:S(2)}, u32[]{:S(2)}) collective-permute-start(bf16[1,4,2,8,128]{4,3,2,1,0:T(8,128)(2,1)} %v0.1), channel_id=1, source_target_pairs={{0,1},{2,3},{4,5},{6,7},{1,0},{3,2},{5,4},{7,6},{8,9},{10,11},{12,... | collective-permute-start | bytes 49160 | tf_op jit(solution)/shard_map/ppermute | solution.py:291
